TPU v7x, 32 devices: a whole 2x2x4 slice. The times are simulated.
32 devices in a mesh: dp: 4 (over z), fsdp: 8 (over y, x, core).
Axes of the slice: x: 2, y: 2, z: 4, core: 2. Of those that a mesh axis runs over, the one named last changes fastest.
Arguments:
- x_in: bfloat16 [192, 256, 512], P(('dp', 'fsdp'))
- positions: int32 [192, 256], P(('dp', 'fsdp'))
- segments: int32 [192, 256], P(('dp', 'fsdp'))
- rel_bias: float32 [32, 6], replicated
- gain_attn: float32 [512], replicated
- gain_mlp: float32 [512], replicated
- w_q: bfloat16 [512, 384], P('fsdp')
- w_k: bfloat16 [512, 384], P('fsdp')
- w_v: bfloat16 [512, 384], P('fsdp')
- w_o: bfloat16 [384, 512], P('fsdp')
- w_i0: bfloat16 [512, 1024], P('fsdp')
- w_i1: bfloat16 [512, 1024], P('fsdp')
- w_f: bfloat16 [1024, 512], P('fsdp')
- grad_out: bfloat16 [192, 256, 512], P(('dp', 'fsdp'))
Outputs:
- output 1: bfloat16 [192, 256, 512], P(('dp', 'fsdp'))
- output 2: float32 [32, 6], replicated
- output 3: float32 [512], replicated
- output 4: float32 [512], replicated
- output 5: bfloat16 [512, 384], P('fsdp')
- output 6: bfloat16 [512, 384], P('fsdp')
- output 7: bfloat16 [512, 384], P('fsdp')
- output 8: bfloat16 [384, 512], P('fsdp')
- output 9: bfloat16 [512, 1024], P('fsdp')
- output 10: bfloat16 [512, 1024], P('fsdp')
- output 11: bfloat16 [1024, 512], P('fsdp')
All inputs are finite; a program needn't handle non-finite values.
Results may differ from a plain program's by a relative error of at most 0.0185089.
Values are sent between devices in bfloat16 or wider.
A program may use at most 1 GiB of HBM per device.

v0:
```python
import jax
import jax.numpy as jnp
from jax import lax
from jax.sharding import PartitionSpec as P

EPSILON = 1e-6
NEG_BIG = -1e9
REL_CLASSES = 32
HALF_CLASSES = 16
EXACT_RANGE = 8
THRESHOLDS = (12, 16, 23, 32, 46, 64, 91)
ROW_AXES = ('dp', 'fsdp')


def rms_norm(values, gain):
    inv_rms = lax.rsqrt(jnp.mean(values * values, axis=-1, keepdims=True) + EPSILON)
    return (values * inv_rms * gain).astype(jnp.bfloat16)


def class_onehot(positions):
    offset = positions[:, None, :] - positions[:, :, None]
    distance = jnp.abs(offset)
    magnitude = jnp.minimum(distance, EXACT_RANGE)
    for bound in THRESHOLDS:
        magnitude = magnitude + (distance >= bound).astype(jnp.int32)
    rel_cls = magnitude + HALF_CLASSES * (offset > 0).astype(jnp.int32)
    return (rel_cls[..., None] == jnp.arange(REL_CLASSES, dtype=jnp.int32)).astype(jnp.float32)


def segment_mask(segments):
    same_seg = segments[:, :, None] == segments[:, None, :]
    return jnp.where(same_seg, 0.0, NEG_BIG).astype(jnp.float32)


def project(tokens_in, weight):
    return jnp.einsum('rsd,de->rse', tokens_in, weight, preferred_element_type=jnp.float32)


def attn_forward(q_all, k_all, v_all, onehot, mask_add, rel_bias):
    bias = jnp.einsum('rqkc,ch->hrqk', onehot, rel_bias, precision=lax.Precision.HIGHEST)
    scores = jnp.einsum('rqhd,rkhd->hrqk', q_all, k_all, preferred_element_type=jnp.float32) + bias + mask_add
    attn_prob = jax.nn.softmax(scores, axis=-1)
    context = jnp.einsum('hrqk,rkhd->rqhd', attn_prob.astype(jnp.bfloat16), v_all, preferred_element_type=jnp.float32)
    return context.astype(jnp.bfloat16), attn_prob


def attn_backward(d_context, q_all, k_all, v_all, attn_prob, onehot):
    prob_low = attn_prob.astype(jnp.bfloat16)
    d_v = jnp.einsum('hrqk,rqhd->rkhd', prob_low, d_context, preferred_element_type=jnp.float32).astype(jnp.bfloat16)
    d_prob = jnp.einsum('rqhd,rkhd->hrqk', d_context, v_all, preferred_element_type=jnp.float32)
    d_scores = attn_prob * (d_prob - jnp.sum(d_prob * attn_prob, axis=-1, keepdims=True))
    d_bias = jnp.einsum('hrqk,rqkc->ch', d_scores, onehot, precision=lax.Precision.HIGHEST)
    d_low = d_scores.astype(jnp.bfloat16)
    d_q = jnp.einsum('hrqk,rkhd->rqhd', d_low, k_all, preferred_element_type=jnp.float32).astype(jnp.bfloat16)
    d_k = jnp.einsum('hrqk,rqhd->rkhd', d_low, q_all, preferred_element_type=jnp.float32).astype(jnp.bfloat16)
    return d_q, d_k, d_v, d_bias


def gather_full(part):
    return lax.all_gather(part, 'fsdp', axis=0, tiled=True)


def reduce_weight(full_grad):
    shard = lax.psum_scatter(full_grad, 'fsdp', scatter_dimension=0, tiled=True)
    return lax.psum(shard, 'dp').astype(jnp.bfloat16)


def local_layer(x_in, positions, segments, rel_bias, gain_attn, gain_mlp, wq_part, wk_part, wv_part, wo_part, wi0_part, wi1_part, wf_part, grad_out):
    w_q = gather_full(wq_part)
    w_k = gather_full(wk_part)
    w_v = gather_full(wv_part)
    w_o = gather_full(wo_part)
    w_i0 = gather_full(wi0_part)
    w_i1 = gather_full(wi1_part)
    w_f = gather_full(wf_part)
    rows, seq_len = x_in.shape[0], x_in.shape[1]
    heads = rel_bias.shape[1]
    x_float = x_in.astype(jnp.float32)
    normed, norm1_pull = jax.vjp(lambda gain: rms_norm(x_float, gain), gain_attn)
    q_all = project(normed, w_q).astype(jnp.bfloat16).reshape(rows, seq_len, heads, -1)
    k_all = project(normed, w_k).astype(jnp.bfloat16).reshape(rows, seq_len, heads, -1)
    v_all = project(normed, w_v).astype(jnp.bfloat16).reshape(rows, seq_len, heads, -1)
    onehot = class_onehot(positions)
    mask_add = segment_mask(segments)
    context, attn_prob = attn_forward(q_all, k_all, v_all, onehot, mask_add, rel_bias)
    context = context.reshape(rows, seq_len, -1)
    hidden = (x_float + project(context, w_o)).astype(jnp.bfloat16)
    h_float = hidden.astype(jnp.float32)
    mlp_in, norm2_pull = jax.vjp(rms_norm, h_float, gain_mlp)
    gate = project(mlp_in, w_i0)
    up_proj = project(mlp_in, w_i1)
    act_float, act_pull = jax.vjp(lambda gate_in, up_in: jax.nn.silu(gate_in) * up_in, gate, up_proj)
    hidden_act = act_float.astype(jnp.bfloat16)
    y_out = (h_float + project(hidden_act, w_f)).astype(jnp.bfloat16)

    d_act = jnp.einsum('rsd,fd->rsf', grad_out, w_f, preferred_element_type=jnp.float32).astype(jnp.bfloat16)
    d_wf = jnp.einsum('rsf,rsd->fd', hidden_act, grad_out, preferred_element_type=jnp.float32)
    d_gate, d_up = act_pull(d_act.astype(jnp.float32))
    d_gate = d_gate.astype(jnp.bfloat16)
    d_up = d_up.astype(jnp.bfloat16)
    d_wi0 = jnp.einsum('rsd,rsf->df', mlp_in, d_gate, preferred_element_type=jnp.float32)
    d_wi1 = jnp.einsum('rsd,rsf->df', mlp_in, d_up, preferred_element_type=jnp.float32)
    d_mlp_in = (jnp.einsum('rsf,df->rsd', d_gate, w_i0, preferred_element_type=jnp.float32)
                + jnp.einsum('rsf,df->rsd', d_up, w_i1, preferred_element_type=jnp.float32)).astype(jnp.bfloat16)
    d_h_norm, d_gain_mlp = norm2_pull(d_mlp_in)
    d_hidden = (grad_out.astype(jnp.float32) + d_h_norm).astype(jnp.bfloat16)
    d_wo = jnp.einsum('rse,rsd->ed', context, d_hidden, preferred_element_type=jnp.float32)
    d_context = jnp.einsum('rsd,ed->rse', d_hidden, w_o, preferred_element_type=jnp.float32).astype(jnp.bfloat16).reshape(rows, seq_len, heads, -1)
    d_q, d_k, d_v, d_bias = attn_backward(d_context, q_all, k_all, v_all, attn_prob, onehot)
    d_q = d_q.reshape(rows, seq_len, -1)
    d_k = d_k.reshape(rows, seq_len, -1)
    d_v = d_v.reshape(rows, seq_len, -1)
    d_wq = jnp.einsum('rsd,rse->de', normed, d_q, preferred_element_type=jnp.float32)
    d_wk = jnp.einsum('rsd,rse->de', normed, d_k, preferred_element_type=jnp.float32)
    d_wv = jnp.einsum('rsd,rse->de', normed, d_v, preferred_element_type=jnp.float32)
    d_normed = (jnp.einsum('rse,de->rsd', d_q, w_q, preferred_element_type=jnp.float32)
                + jnp.einsum('rse,de->rsd', d_k, w_k, preferred_element_type=jnp.float32)
                + jnp.einsum('rse,de->rsd', d_v, w_v, preferred_element_type=jnp.float32)).astype(jnp.bfloat16)
    d_gain_attn = norm1_pull(d_normed)[0]
    return (y_out, lax.psum(d_bias, ROW_AXES), lax.psum(d_gain_attn, ROW_AXES), lax.psum(d_gain_mlp, ROW_AXES),
            reduce_weight(d_wq), reduce_weight(d_wk), reduce_weight(d_wv), reduce_weight(d_wo),
            reduce_weight(d_wi0), reduce_weight(d_wi1), reduce_weight(d_wf))


def solution(mesh):
    row_spec = P(ROW_AXES)
    whole = P()
    part_spec = P('fsdp')
    in_specs = (row_spec, row_spec, row_spec, whole, whole, whole) + (part_spec,) * 7 + (row_spec,)
    out_specs = (row_spec, whole, whole, whole) + (part_spec,) * 7
    return jax.shard_map(local_layer, mesh=mesh, in_specs=in_specs, out_specs=out_specs, check_vma=False)
```

profile of v0, /device:TPU:0, one launch (start us, length us, event | category | flops | bytes accessed | tf_op | source)
XLA Modules:
  0.0 488.9 jit_solution(1528247070201592087)
XLA Ops:
  12.1 12.8 %all_gather.22 = bf16[512,384]{1,0:T(8,128)(2,1)} all-gather(bf16[64,384]{1,0:T(8,128)(2,1)} %param.20), channel_id=1, replica_groups=mesh['dp'=4,'fsdp'=8] {'fsdp'}, dimensions={0}, use_global_device_ids=true | all-gather | bytes 442368 | tf_op jit(solution)/shard_map/all_gather | solution.py:60
  24.9 9.8 %all_gather.23 = bf16[512,384]{1,0:T(8,128)(2,1)S(1)} all-gather(bf16[64,384]{1,0:T(8,128)(2,1)} %param.21), channel_id=1, replica_groups=mesh['dp'=4,'fsdp'=8] {'fsdp'}, dimensions={0}, use_global_device_ids=true | all-gather | bytes 442368 | tf_op jit(solution)/shard_map/all_gather | solution.py:60
  34.7 9.4 %all_gather.21 = bf16[512,384]{1,0:T(8,128)(2,1)S(1)} all-gather(bf16[64,384]{1,0:T(8,128)(2,1)} %param.22), channel_id=1, replica_groups=mesh['dp'=4,'fsdp'=8] {'fsdp'}, dimensions={0}, use_global_device_ids=true | all-gather | bytes 442368 | tf_op jit(solution)/shard_map/all_gather | solution.py:60
  44.1 9.4 %all_gather.24 = bf16[384,512]{1,0:T(8,128)(2,1)} all-gather(bf16[48,512]{1,0:T(8,128)(2,1)S(1)} %copy-done.26), channel_id=1, replica_groups=mesh['dp'=4,'fsdp'=8] {'fsdp'}, dimensions={0}, use_global_device_ids=true | all-gather | bytes 442368 | tf_op jit(solution)/shard_map/all_gather | solution.py:60
  55.6 2.4 copy.54
  61.7 3.1 convolution_convert_fusion.3
  69.6 15.7 %fusion.1 = f32[6,256,256,6]{1,3,2,0:T(8,128)S(1)} fusion(f32[32,6]{0,1:T(8,128)S(1)} %copy-done, s32[6,256,256]{1,0,2:T(8,128)S(1)} %fusion.49), kind=kOutput, calls=%fused_computation.2 | convolution fusion | flops 918552576 | bytes 11010816 | tf_op jit(solution)/shard_map/rqkc,ch->hrqk/dot_general | solution.py:40
  85.2 7.1 %fusion.5 = f32[6,6,256,256]{2,3,1,0:T(8,128)} fusion(f32[6,256,256,6]{1,3,2,0:T(8,128)S(1)} %fusion.1, f32[6,256,256]{1,2,0:T(8,128)S(1)} %compare_select_fusion, bf16[6,256,6,64]{1,3,2,0:T(8,128)(2,1)S(1)} %bitcast.107, bf16[6,256,6,64]{1,3,2,0:T(8,128)(2,1)S(1)} %bitcast.109), kind=kOutput, calls=%fused_computation.8 | convolution fusion | flops 306708480 | bytes 22806528 | tf_op jit(solution)/shard_map/rqhd,rkhd->hrqk/dot_general | solution.py:41
  92.4 8.1 %fusion.103 = (f32[6,6,256]{2,1,0:T(8,128)S(1)}, f32[6,6,256,256]{2,3,1,0:T(8,128)S(1)}) fusion(f32[6,6,256,256]{2,3,1,0:T(8,128)} %fusion.5), kind=kOutput, calls=%fused_computation.125 | output fusion | flops 4718847 | bytes 18911232 | tf_op jit(solution)/shard_map/sub | solution.py:42
  104.0 3.2 fusion.50
  109.9 5.2 %convolution_convert_fusion = bf16[6,256,1024]{2,1,0:T(8,128)(2,1)} fusion(bf16[6,256,512]{2,1,0:T(8,128)(2,1)} %param.27, bf16[1024,512]{1,0:T(8,128)(2,1)} %all-gather.8.cloned.1.call-done), kind=kOutput, calls=%fused_computation.68 | convolution fusion | flops 1612185600 | bytes 5767168 | tf_op jit(solution)/shard_map/rsd,fd->rsf/dot_general | solution.py:96
  115.1 6.1 %fusion.73 = f32[6,256,1024]{2,1,0:T(8,128)} fusion(bf16[512,1024]{1,0:T(8,128)(2,1)} %all-gather.6.cloned.1.call-done, bf16[6,256,512]{2,1,0:T(8,128)(2,1)} %get-tuple-element.31, f32[512]{0:T(512)S(1)} %copy-done.29, f32[6,256]{1,0:T(8,128)S(1)} %fusion.93), kind=kOutput, calls=%fused_computation.102 | convolution fusion | flops 1613758464 | bytes 8921088 | tf_op jit(solution)/shard_map/rsd,de->rse/dot_general | solution.py:36
  121.2 9.2 %fusion.9 = (bf16[6,256,1024]{2,1,0:T(8,128)(2,1)S(1)}, bf16[6,256,1024]{2,1,0:T(8,128)(2,1)}, bf16[6,256,1024]{2,1,0:T(8,128)(2,1)S(1)}) fusion(f32[6,256,1024]{2,1,0:T(8,128)} %fusion.73, bf16[6,256,1024]{2,1,0:T(8,128)(2,1)} %convolution_convert_fusion, bf16[512,1024]{1,0:T(8,128)(2,1)} %all-gather.4.cloned.1.call-done, ...), kind=kOutput, calls=%fused_computation.17 | convolution fusion | flops 1640497152 | bytes 21504000 | tf_op jit(solution)/shard_map/rsd,de->rse/dot_general | solution.py:36
  134.1 2.9 fusion.26
  141.0 3.5 convolution_convert_fusion.1
  146.9 5.3 %fusion.53 = bf16[6,6,64,256]{3,2,1,0:T(8,128)(2,1)} fusion(bf16[6,256,6,64]{1,3,2,0:T(8,128)(2,1)} %bitcast.115, bf16[6,6,256,256]{2,3,1,0:T(8,128)(2,1)} %copy-done.4), kind=kOutput, calls=%fused_computation.82 | convolution fusion | flops 302579712 | bytes 7077888 | tf_op jit(solution)/shard_map/hrqk,rqhd->rkhd/dot_general | solution.py:49
  152.3 4.0 convolution_bitcast_fusion.4
  156.3 9.6 %multiply_reduce_fusion = (f32[6,6,256]{2,1,0:T(8,128)S(1)}, f32[6,6,256,256]{2,3,1,0:T(8,128)}) fusion(f32[6,6,256,256]{2,3,1,0:T(8,128)} %copy-done.2, f32[6,6,256]{2,1,0:T(8,128)S(1)} %get-tuple-element.28, bf16[6,256,6,64]{1,3,2,0:T(8,128)(2,1)} %bitcast.114, bf16[6,256,6,64]{1,3,2,0:T(8,128)(2,1)} %bitcast.116), kind=kOutput, calls=%fused_computation.10 | convolution fusion | flops 309058560 | bytes 21307392 | tf_op jit(solution)/shard_map/rqhd,rkhd->hrqk/dot_general | solution.py:50
  166.0 11.4 %fusion.102 = (bf16[6,6,256,256]{2,3,1,0:T(8,128)(2,1)S(1)}, f32[6,6,256,256]{2,3,1,0:T(8,128)}) fusion(f32[6,6,256,256]{2,3,1,0:T(8,128)} %get-tuple-element.34, f32[6,6,256]{2,1,0:T(8,128)S(1)} %get-tuple-element.33, f32[6,6,256,256]{2,3,1,0:T(8,128)} %copy-done.2, f32[6,6,256]{2,1,0:T(8,128)S(1)} %get-tuple-element.28), kind=kLoop, calls=%fused_computation.124 | loop fusion | flops 9437184 | bytes 33103872 | tf_op jit(solution)/shard_map/convert_element_type | solution.py:53
  182.9 3.4 fusion.56
  189.7 5.5 %convolution_bitcast_fusion = f32[1024,512]{1,0:T(8,128)} fusion(bf16[6,256,1024]{2,1,0:T(8,128)(2,1)} %get-tuple-element.26, bf16[6,256,512]{2,1,0:T(8,128)(2,1)} %param.27), kind=kOutput, calls=%fused_computation.77 | convolution fusion | flops 1610612736 | bytes 6815744 | tf_op jit(solution)/shard_map/rsf,rsd->fd/dot_general | solution.py:97
  195.3 5.6 %convolution_bitcast_fusion.1 = f32[512,1024]{1,0:T(8,128)} fusion(bf16[6,256,1024]{2,1,0:T(8,128)(2,1)} %copy-done.35, bf16[6,256,512]{2,1,0:T(8,128)(2,1)} %get-tuple-element.31, f32[512]{0:T(512)S(1)} %copy-done.29, f32[6,256]{1,0:T(8,128)S(1)} %fusion.93), kind=kOutput, calls=%fused_computation.78 | convolution fusion | flops 1613758464 | bytes 6823936 | tf_op jit(solution)/shard_map/rsd,rsf->df/dot_general | solution.py:102
  201.0 5.7 %convolution_bitcast_fusion.2 = f32[512,1024]{1,0:T(8,128)} fusion(bf16[6,256,1024]{2,1,0:T(8,128)(2,1)} %copy-done.34, bf16[6,256,512]{2,1,0:T(8,128)(2,1)} %get-tuple-element.31, f32[512]{0:T(512)S(1)} %copy-done.29, f32[6,256]{1,0:T(8,128)S(1)} %fusion.93), kind=kOutput, calls=%fused_computation.79 | convolution fusion | flops 1613758464 | bytes 6823936 | tf_op jit(solution)/shard_map/rsd,rsf->df/dot_general | solution.py:101
  206.8 2.5 fusion.88
  212.7 28.9 %fusion.67 = f32[32,6]{0,1:T(8,128)S(1)} fusion(f32[6,6,256,256]{2,3,1,0:T(8,128)} %get-tuple-element.24, s32[6,256,256]{1,0,2:T(8,128)S(1)} %fusion.49), kind=kOutput, calls=%fused_computation.98 | convolution fusion | flops 918552576 | bytes 11010816 | tf_op jit(solution)/shard_map/hrqk,rqkc->ch/dot_general | solution.py:52
  241.6 39.7 %all-reduce = (f32[32,6]{0,1:T(8,128)}, f32[512]{0:T(512)}, f32[512]{0:T(512)}) all-reduce(f32[32,6]{0,1:T(8,128)S(1)} %fusion.67, f32[512]{0:T(512)S(1)} %fusion.25, f32[512]{0:T(512)S(1)} %get-tuple-element.11), channel_id=1, replica_groups=mesh['dp'=4,'fsdp'=8] {'dp','fsdp'}, use_global_device_ids=true, to_apply=%region_6.7 | all-reduce | flops 1216 | bytes 9728 | tf_op jit(solution)/shard_map/psum | solution.py:120
  281.3 5.3 %fusion.32 = bf16[6,256,512]{2,1,0:T(8,128)(2,1)} fusion(bf16[6,256,512]{2,1,0:T(8,128)(2,1)} %get-tuple-element.31, bf16[6,256,1024]{2,1,0:T(8,128)(2,1)} %get-tuple-element.26, bf16[1024,512]{1,0:T(8,128)(2,1)S(1)} %copy-done.30), kind=kOutput, calls=%fused_computation.54 | convolution fusion | flops 1612972032 | bytes 7340032 | tf_op jit(solution)/shard_map/rsd,de->rse/dot_general | solution.py:36
  286.6 14.8 %reduce-scatter.8.cloned.1.call-done = f32[64,384]{1,0:T(8,128)} async-done(((f32[512,384]{1,0:T(8,128)}), f32[64,384]{1,0:T(8,128)}) %reduce-scatter.8.cloned.1.call-update) | async-done | bytes 98320 | tf_op jit(solution)/shard_map/reduce_scatter | solution.py:64
  301.4 44.2 %reduce-scatter.20.cloned.1.call-done = f32[128,512]{1,0:T(8,128)} async-done(((f32[1024,512]{1,0:T(8,128)}), f32[128,512]{1,0:T(8,128)}) %reduce-scatter.20.cloned.1.call-update) | async-done | bytes 262160 | tf_op jit(solution)/shard_map/reduce_scatter | solution.py:64
  345.6 44.2 %reduce-scatter.18.cloned.1.call-done = f32[64,1024]{1,0:T(8,128)} async-done(((f32[512,1024]{1,0:T(8,128)}), f32[64,1024]{1,0:T(8,128)}) %reduce-scatter.18.cloned.1.call-update) | async-done | bytes 262160 | tf_op jit(solution)/shard_map/reduce_scatter | solution.py:64
  389.9 44.1 %reduce-scatter.16.cloned.1.call-done = f32[64,1024]{1,0:T(8,128)} async-done(((f32[512,1024]{1,0:T(8,128)}), f32[64,1024]{1,0:T(8,128)}) %reduce-scatter.16.cloned.1.call-update) | async-done | bytes 262160 | tf_op jit(solution)/shard_map/reduce_scatter | solution.py:64
  433.9 47.9 %all-reduce.3 = (bf16[64,384]{1,0:T(8,128)(2,1)}, bf16[64,384]{1,0:T(8,128)(2,1)}, bf16[64,384]{1,0:T(8,128)(2,1)}, bf16[48,512]{1,0:T(8,128)(2,1)}, bf16[64,102...) all-reduce(f32[64,384]{1,0:T(8,128)} %reduce-scatter.8.cloned.1.cal, ...), channel_id=1, replica_groups=mesh['dp'=4,'fsdp'=8] {'dp'}, use_global_device_ids=true, to_apply=%region_12.13 | all-reduce | flops 294912 | bytes 1769472 | tf_op jit(solution)/shard_map/psum | solution.py:65
  (120 shorter events, 43.9 us)
Async XLA Ops:
  7.2 62.4 %copy-start = (f32[32,6]{0,1:T(8,128)S(1)}, f32[32,6]{0,1:T(8,128)}, u32[]{:S(2)}) copy-start(f32[32,6]{0,1:T(8,128)} %param.17) | copy-start | bytes 2308
  7.2 46.4 %copy-start.7 = (bf16[6,256,512]{2,1,0:T(8,128)(2,1)S(1)}, bf16[6,256,512]{2,1,0:T(8,128)(2,1)}, u32[]{:S(2)}) copy-start(bf16[6,256,512]{2,1,0:T(8,128)(2,1)} %param.14) | copy-start | bytes 4718596
  7.2 36.9 %copy-start.26 = (bf16[48,512]{1,0:T(8,128)(2,1)S(1)}, bf16[48,512]{1,0:T(8,128)(2,1)}, u32[]{:S(2)}) copy-start(bf16[48,512]{1,0:T(8,128)(2,1)} %param.23) | copy-start | bytes 147460
  7.2 46.4 %copy-start.33 = (f32[512]{0:T(512)S(1)}, f32[512]{0:T(512)}, u32[]{:S(2)}) copy-start(f32[512]{0:T(512)} %param.18) | copy-start | bytes 6148
  7.2 102.6 %all-gather.8.cloned.1.call-start = ((), (), s32[]{:S(2)}) async-start(), calls=%async_computation.9 | async-start | bytes 1179648 | tf_op jit(solution)/shard_map/all_gather | solution.py:60
  8.0 107.1 %all-gather.6.cloned.1.call-start = ((), (), s32[]{:S(2)}) async-start(), calls=%async_computation.8 | async-start | bytes 1179648 | tf_op jit(solution)/shard_map/all_gather | solution.py:60
  8.7 112.5 %all-gather.4.cloned.1.call-start = ((), (), s32[]{:S(2)}) async-start(), calls=%async_computation.7 | async-start | bytes 1179648 | tf_op jit(solution)/shard_map/all_gather | solution.py:60
  9.4 277.2 %reduce-scatter.14.cloned.1.call-start = ((), (), s32[]{:S(2)}) async-start(), calls=%async_computation.13 | async-start | bytes 884736 | tf_op jit(solution)/shard_map/reduce_scatter | solution.py:64
  34.7 23.3 %copy-start.18 = (bf16[512,384]{1,0:T(8,128)(2,1)}, bf16[512,384]{1,0:T(8,128)(2,1)S(1)}, u32[]{:S(2)}) copy-start(bf16[512,384]{1,0:T(8,128)(2,1)S(1)} %all_gather.23) | copy-start | bytes 1179652
  44.1 13.9 %copy-start.16 = (bf16[512,384]{1,0:T(8,128)(2,1)}, bf16[512,384]{1,0:T(8,128)(2,1)S(1)}, u32[]{:S(2)}) copy-start(bf16[512,384]{1,0:T(8,128)(2,1)S(1)} %all_gather.21) | copy-start | bytes 1179652
  61.7 5.5 %copy-start.27 = (s32[6,256]{1,0:T(8,128)S(1)}, s32[6,256]{1,0:T(8,128)}, u32[]{:S(2)}) copy-start(s32[6,256]{1,0:T(8,128)} %param.16) | copy-start | bytes 18436
  69.5 15.7 %copy-start.5 = (bf16[6,256,384]{1,2,0:T(8,128)(2,1)S(1)}, bf16[6,256,384]{1,2,0:T(8,128)(2,1)}, u32[]{:S(2)}) copy-start(bf16[6,256,384]{1,2,0:T(8,128)(2,1)} %copy.55) | copy-start | bytes 3538948
  100.4 3.6 copy-start.2
  104.0 3.2 copy-start.4
  104.0 3.5 copy-start.8
  104.0 3.5 copy-start.25
  109.8 5.3 %copy-start.29 = (f32[512]{0:T(512)S(1)}, f32[512]{0:T(512)}, u32[]{:S(2)}) copy-start(f32[512]{0:T(512)} %param.19) | copy-start | bytes 6148
  121.2 9.2 %copy-start.32 = (bf16[512,1024]{1,0:T(8,128)(2,1)S(1)}, bf16[512,1024]{1,0:T(8,128)(2,1)}, u32[]{:S(2)}) copy-start(bf16[512,1024]{1,0:T(8,128)(2,1)} %all-gather.4.cloned.1.call-done) | copy-start | bytes 3145732
  130.4 3.0 copy-start.35
  130.5 3.0 copy-start.21
  130.5 3.7 copy-start.31
  152.2 134.4 %reduce-scatter.12.cloned.1.call-start = ((), (), s32[]{:S(2)}) async-start(), calls=%async_computation.12 | async-start | bytes 884736 | tf_op jit(solution)/shard_map/reduce_scatter | solution.py:64
  165.9 120.7 %reduce-scatter.10.cloned.1.call-start = ((), (), s32[]{:S(2)}) async-start(), calls=%async_computation.11 | async-start | bytes 884736 | tf_op jit(solution)/shard_map/reduce_scatter | solution.py:64
  166.0 11.4 %copy-start.6 = (bf16[6,256,384]{1,2,0:T(8,128)(2,1)S(1)}, bf16[6,256,384]{1,2,0:T(8,128)(2,1)}, u32[]{:S(2)}) copy-start(bf16[6,256,384]{1,2,0:T(8,128)(2,1)} %copy.55) | copy-start | bytes 3538948
  177.4 3.2 copy-start.9
  182.8 118.6 %reduce-scatter.8.cloned.1.call-start = ((), (), s32[]{:S(2)}) async-start(), calls=%async_computation.10 | async-start | bytes 884736 | tf_op jit(solution)/shard_map/reduce_scatter | solution.py:64
  182.9 4.4 copy-start.10
  189.7 156.0 %reduce-scatter.20.cloned.1.call-start = ((), (), s32[]{:S(2)}) async-start(), calls=%async_computation.16 | async-start | bytes 2359296 | tf_op jit(solution)/shard_map/reduce_scatter | solution.py:64
  195.3 194.6 %reduce-scatter.18.cloned.1.call-start = ((), (), s32[]{:S(2)}) async-start(), calls=%async_computation.15 | async-start | bytes 2359296 | tf_op jit(solution)/shard_map/reduce_scatter | solution.py:64
  201.0 233.0 %reduce-scatter.16.cloned.1.call-start = ((), (), s32[]{:S(2)}) async-start(), calls=%async_computation.14 | async-start | bytes 2359296 | tf_op jit(solution)/shard_map/reduce_scatter | solution.py:64
  212.7 68.6 %copy-start.30 = (bf16[1024,512]{1,0:T(8,128)(2,1)S(1)}, bf16[1024,512]{1,0:T(8,128)(2,1)}, u32[]{:S(2)}) copy-start(bf16[1024,512]{1,0:T(8,128)(2,1)} %all-gather.8.cloned.1.call-done) | copy-start | bytes 3145732
  281.3 200.5 %copy-start.1 = (f32[32,6]{0,1:T(8,128)S(1)}, f32[32,6]{0,1:T(8,128)}, u32[]{:S(2)}) copy-start(f32[32,6]{0,1:T(8,128)} %param.17) | copy-start | bytes 2308
  (14 other events, 27.7 us)
Sparse Core Ops, SparseCore 0:
  9.9 26.8 all-gather.7
  38.7 23.5 all-gather.5
  64.2 23.1 all-gather.3
  152.4 35.1 reduce-scatter.13
  190.5 34.8 reduce-scatter.11
  228.4 34.9 reduce-scatter.9
  266.5 34.8 reduce-scatter.7
  304.7 40.8 reduce-scatter.19
  348.9 40.8 reduce-scatter.17
  393.0 40.8 reduce-scatter.15
where the time goes:
time: 497 us; the launch traced here: 489 us
  matrix products  151 us (30%)
  waiting for transfers between devices  150 us (30%)
  blocking collectives  129 us (26%)
  other arithmetic  26 us (5%)
  local copies, waits for them, and re-layouts  18.6 us (4%)
  between operations  14.8 us (3%)
    reduce_scatter x7, waiting for transfers between devices, reduce_weight(): shard = lax.psum_scatter(full_grad, 'fsdp', scatter_dimension=0, tiled=True)  147 us
    psum x1, blocking collectives, reduce_weight(): return lax.psum(shard, 'dp').astype(jnp.bfloat16)  47.9 us
    all_gather x4, blocking collectives, gather_full(): return lax.all_gather(part, 'fsdp', axis=0, tiled=True)  41.4 us
    psum x1, blocking collectives, local_layer(): lax.psum(d_bias, ROW_AXES)  39.7 us
    dot_general x7, matrix products, project(): jnp.einsum('rsd,de->rse', tokens_in, weight, preferred_element_type=jnp.f...  30.1 us
    dot_general x1, matrix products, attn_backward(): jnp.einsum('hrqk,rqkc->ch', d_scores, onehot, precision=lax.Precision.HIG...  28.9 us
    dot_general x1, matrix products, attn_forward(): jnp.einsum('rqkc,ch->hrqk', onehot, rel_bias, precision=lax.Precision.HIG...  15.7 us
    convert_element_type x1, other arithmetic, attn_backward(): d_low = d_scores.astype(jnp.bfloat16)  11.4 us
  transfers between devices with their start and end apart: 10, of which 4 were waited for; matrix products, arithmetic and copies ran while one was open for 32% of the time, Pallas kernels for 0%

commit v1 on v0

v1 whole, which is shorter than its diff:
```python
import functools

import jax
import jax.numpy as jnp
from jax import lax
from jax.experimental import pallas as pl
from jax.experimental.pallas import tpu as pltpu
from jax.sharding import PartitionSpec as P

EPSILON = 1e-6
NEG_BIG = -1e9
THRESHOLDS = (12, 16, 23, 32, 46, 64, 91)
ROW_AXES = ('dp', 'fsdp')
ROWS, SEQ, DM, HEADS, HD, FF = 6, 256, 512, 6, 64, 1024
TOK = ROWS * SEQ
AW = HEADS * HD
F32, BF16 = jnp.float32, jnp.bfloat16


def mm(a, b):
    return lax.dot_general(a, b, (((1,), (0,)), ((), ())), preferred_element_type=F32)


def mm_nt(a, b):
    return lax.dot_general(a, b, (((1,), (1,)), ((), ())), preferred_element_type=F32)


def mm_tn(a, b):
    return lax.dot_general(a, b, (((0,), (0,)), ((), ())), preferred_element_type=F32)


def split3(v):
    hi = v.astype(BF16)
    rest = v - hi.astype(F32)
    mid = rest.astype(BF16)
    lo = (rest - mid.astype(F32)).astype(BF16)
    return hi, mid, lo


def tok_slice(r):
    return pl.ds(pl.multiple_of(r * SEQ, SEQ), SEQ)


def rel_class(diff):
    m = jnp.abs(diff)
    e = jnp.minimum(m, 8.0)
    for bound in THRESHOLDS:
        e = e + jnp.where(m >= bound, 1.0, 0.0)
    return e + jnp.where(diff > 0, 16.0, 0.0)


def setup_small(relb_ref, ga_ref, gm_ref, tab_s, pad_s, ga_s, gm_s):
    pad_s[...] = jnp.zeros_like(pad_s)
    pad_s[0:32, 0:HEADS] = relb_ref[...]
    t = pad_s[...].T[0:8, :]
    lane = lax.broadcasted_iota(jnp.int32, t.shape, 1)
    tab_s[...] = jnp.where(lane < 32, t, pltpu.roll(t, 32, 1) + NEG_BIG)
    ga_s[...] = jnp.broadcast_to(ga_ref[...], (128, DM)).T
    gm_s[...] = jnp.broadcast_to(gm_ref[...], (128, DM)).T


def wide(col128):
    return jnp.concatenate([col128, col128], axis=1)


def attn_fwd_row(r, x_ref, pos_ref, seg_ref, tab_s, ga_s, wqkvt_s, xt_s, qkv_s, p_s, ctx_s):
    tok = tok_slice(r)
    xt = x_ref[pl.ds(pl.multiple_of(r * SEQ, SEQ), SEQ), :].T
    xt_s[:, tok] = xt
    xf = xt.astype(F32)
    inv = lax.rsqrt(jnp.mean(xf * xf, axis=0, keepdims=True) + EPSILON)
    at = (xf * inv * wide(ga_s[...])).astype(BF16)
    qkv_s[:, tok] = mm(wqkvt_s[...], at).astype(BF16)
    code = (seg_ref[r] * 1024 + pos_ref[r]).astype(F32)
    code = jnp.broadcast_to(code, (SEQ, SEQ))
    diff = code.T - code
    idx = (rel_class(diff) + jnp.where(jnp.abs(diff) >= 512.0, 32.0, 0.0)).astype(jnp.int32)
    for h in range(HEADS):
        qt = qkv_s[h * HD:(h + 1) * HD, tok]
        kt = qkv_s[AW + h * HD:AW + (h + 1) * HD, tok]
        vt = qkv_s[2 * AW + h * HD:2 * AW + (h + 1) * HD, tok]
        table = jnp.broadcast_to(tab_s[h:h + 1, :], (SEQ, 128))
        bias = jnp.concatenate([jnp.take_along_axis(table, idx[:, 0:128], axis=1),
                                jnp.take_along_axis(table, idx[:, 128:256], axis=1)], axis=1)
        s = mm_tn(kt, qt) + bias
        p = jnp.exp(s - jnp.max(s, axis=0, keepdims=True))
        p = p * (1.0 / jnp.sum(p, axis=0, keepdims=True))
        p_s[h, r] = p
        ctx_s[h * HD:(h + 1) * HD, tok] = mm(vt, p.astype(BF16)).astype(BF16)


def mlp_row(r, go_ref, y_ref, gm_s, wot_s, wit_s, wft_s, wi_s, wf_s, xt_s, ctx_s, got_s, ut_s, zt_s, dgu_s, dh_s, dgm_s):
    tok = tok_slice(r)
    rows = pl.ds(pl.multiple_of(r * SEQ, SEQ), SEQ)
    ht = (xt_s[:, tok].astype(F32) + mm(wot_s[...], ctx_s[:, tok])).astype(BF16)
    hf = ht.astype(F32)
    inv = lax.rsqrt(jnp.mean(hf * hf, axis=0, keepdims=True) + EPSILON)
    gm = wide(gm_s[...])
    ut = (hf * inv * gm).astype(BF16)
    ut_s[:, tok] = ut
    got = go_ref[rows, :].T
    got_s[:, tok] = got
    step = 256
    for f in range(0, FF, step):
        gate = mm(wit_s[f:f + step, :], ut)
        up = mm(wit_s[FF + f:FF + f + step, :], ut)
        dz = mm(wf_s[f:f + step, :], got).astype(BF16).astype(F32)
        sg = 1.0 / (1.0 + jnp.exp(-gate))
        silu = gate * sg
        zt_s[f:f + step, tok] = (silu * up).astype(BF16)
        dgu_s[f:f + step, tok] = (dz * up * (sg * (1.0 + gate * (1.0 - sg)))).astype(BF16)
        dgu_s[FF + f:FF + f + step, tok] = (dz * silu).astype(BF16)
    yt = (hf + mm(wft_s[...], zt_s[:, tok])).astype(BF16)
    y_ref[rows, :] = yt.T
    du = mm(wi_s[...], dgu_s[:, tok]).astype(BF16).astype(F32)
    hn = hf * inv
    dg = du * hn
    dgm_s[...] += dg[:, 0:128] + dg[:, 128:256]
    dug = du * gm
    dhn = inv * (dug - hn * jnp.mean(dug * hn, axis=0, keepdims=True))
    dh_s[:, tok] = (got.astype(F32) + dhn).astype(BF16)


def attn_bwd_row(r, pos_ref, ga_s, wqkv_s, wo_s, xt_s, at_s, qkv_s, p_s, dh_s, dqkv_s, dacc_s, dga_s):
    tok = tok_slice(r)
    dct = mm(wo_s[...], dh_s[:, tok]).astype(BF16)
    pos = pos_ref[r]
    onehot = jnp.where(lax.broadcasted_iota(jnp.int32, (SEQ, SEQ), 0) == pos, 1.0, 0.0).astype(BF16)
    for h in range(HEADS):
        qt = qkv_s[h * HD:(h + 1) * HD, tok]
        kt = qkv_s[AW + h * HD:AW + (h + 1) * HD, tok]
        vt = qkv_s[2 * AW + h * HD:2 * AW + (h + 1) * HD, tok]
        dc = dct[h * HD:(h + 1) * HD, :]
        p = p_s[h, r]
        dp = mm_tn(vt, dc)
        ds = p * (dp - jnp.sum(dp * p, axis=0, keepdims=True))
        dqkv_s[2 * AW + h * HD:2 * AW + (h + 1) * HD, tok] = mm_nt(dc, p.astype(BF16)).astype(BF16)
        hi, mid, lo = split3(ds)
        dqkv_s[h * HD:(h + 1) * HD, tok] = mm(kt, hi).astype(BF16)
        dqkv_s[AW + h * HD:AW + (h + 1) * HD, tok] = mm_nt(qt, hi).astype(BF16)
        t = mm(onehot, hi) + mm(onehot, mid) + mm(onehot, lo)
        hi, mid, lo = split3(t)
        dacc_s[h] += mm_nt(hi, onehot) + mm_nt(mid, onehot) + mm_nt(lo, onehot)
    dn = mm(wqkv_s[...], dqkv_s[0:3 * AW, tok]).astype(BF16).astype(F32)
    xf = xt_s[:, tok].astype(F32)
    inv = lax.rsqrt(jnp.mean(xf * xf, axis=0, keepdims=True) + EPSILON)
    xn = xf * inv
    at_s[:, tok] = (xn * wide(ga_s[...])).astype(BF16)
    dg = dn * xn
    dga_s[...] += dg[:, 0:128] + dg[:, 128:256]


def bias_sums(dacc_s, db_s):
    db_s[...] = jnp.zeros_like(db_s)
    diff = (lax.broadcasted_iota(jnp.int32, (SEQ, SEQ), 0) - lax.broadcasted_iota(jnp.int32, (SEQ, SEQ), 1)).astype(F32)
    cls = rel_class(diff)

    def body(c, carry):
        hit = cls == c.astype(F32)
        for h in range(HEADS):
            db_s[pl.ds(c * 8 + h, 1), :] = jnp.sum(jnp.where(hit, dacc_s[h], 0.0), axis=0, keepdims=True)
        return carry
    lax.fori_loop(0, 32, body, 0)


def loop(n, fn):
    def body(i, carry):
        fn(i)
        return carry
    lax.fori_loop(0, n, body, 0)


MESH = pl.DeviceIdType.MESH
SHARD = ((128, 512), (64, 2048), (48, 512), (64, 1152))
WF, WI, WO, WQKV = 0, 1, 2, 3
NSEM = 16


def remote(src, dst, send, recv, i, dev):
    return pltpu.make_async_remote_copy(src_ref=src, dst_ref=dst, send_sem=send.at[i], recv_sem=recv.at[i],
                                        device_id=dev, device_id_type=MESH)


class Place:
    def __init__(self):
        self.f = lax.axis_index('fsdp')
        self.z = lax.axis_index('dp')
        self.c = lax.rem(self.f, 2)
        self.k = self.f // 2
        self.x = lax.rem(self.k, 2)
        self.y = self.k // 2
        self.kx = self.k + 1 - 2 * self.x
        self.ky = self.k + 2 - 4 * self.y
        self.kd = 3 - self.k
        self.sib = {'fsdp': self.f + 1 - 2 * self.c}
        self.nx = {'fsdp': 2 * self.kx + self.c}
        self.ny = {'fsdp': 2 * self.ky + self.c}
        self.nd = {'fsdp': 2 * self.kd + self.c}
        self.up = [lax.rem(self.z + j, 4) for j in (1, 2, 3)]
        self.nz = [{'dp': u} for u in self.up]


class Gather:
    def __init__(self, at, parts, fulls, own, send, recv):
        self.at, self.parts, self.fulls, self.own, self.send, self.recv = at, parts, fulls, own, send, recv

    def view(self, w, f):
        full, col = self.fulls[w]
        rows, cols = self.parts[w].shape
        return full.at[pl.ds(pl.multiple_of(f * rows, rows), rows), pl.ds(col, cols)]

    def load(self, w):
        return pltpu.make_async_copy(self.parts[w], self.view(w, self.at.f), self.own.at[w])

    def direct(self, w, j):
        at = self.at
        v = self.view(w, at.f)
        return remote(v, v, self.send, self.recv, w * 7 + j, (at.nx, at.ny, at.nd, at.sib)[j])

    def forward(self, w, j):
        at = self.at
        v = self.view(w, 2 * (at.kx, at.ky, at.kd)[j] + at.c)
        return remote(v, v, self.send, self.recv, w * 7 + 4 + j, at.sib)

    def begin(self, ws):
        for w in ws:
            self.load(w).wait()
            for j in (2, 0, 1, 3):
                self.direct(w, j).start()

    def relay(self, ws):
        for w in ws:
            for j in (0, 1, 2):
                self.direct(w, j).wait_recv()
                self.forward(w, j).start()

    def finish(self, ws):
        for w in ws:
            self.direct(w, 3).wait_recv()
            for j in (0, 1, 2):
                self.forward(w, j).wait_recv()

    def drain(self):
        for w in range(len(self.parts)):
            for j in range(4):
                self.direct(w, j).wait_send()
            for j in range(3):
                self.forward(w, j).wait_send()


class Reduce:
    def __init__(self, a, at, acc, rd, r1, r2, rz, out, send, recv):
        self.a, self.at, self.acc, self.rd, self.r1, self.r2, self.rz, self.out = a, at, acc, rd, r1, r2, rz, out
        self.send, self.recv = send, recv
        self.rows, self.cols = SHARD[a]
        self.half = self.rows // 2

    def part(self, k, c, h=None):
        n = self.rows if h is None else self.half
        off = (2 * k + c) * self.rows + (0 if h is None else h * self.half)
        return self.acc.at[pl.ds(pl.multiple_of(off, 8), n), :]

    def copy(self, src, dst, i, dev):
        return remote(src, dst, self.send, self.recv, self.a * NSEM + i, dev)

    def d_copy(self, i):
        at = self.at
        k = (at.kd, at.kx, at.ky, at.k)[i]
        return self.copy(self.part(k, 1 - at.c), self.rd.at[i], i, at.sib)

    def xy1_copy(self, i):
        at = self.at
        k, h, dev = ((at.kx, 0, at.nx), (at.kd, 0, at.nx), (at.ky, 1, at.ny), (at.kd, 1, at.ny))[i]
        return self.copy(self.part(k, at.c, h), self.r1.at[i], 4 + i, dev)

    def xy2_copy(self, i):
        at = self.at
        k, h, dev = ((at.ky, 0, at.ny), (at.kx, 1, at.nx))[i]
        return self.copy(self.part(k, at.c, h), self.r2.at[i], 8 + i, dev)

    def quarter(self, z, base):
        if self.rows == 48:
            return pl.ds(base, self.rows), pl.ds(pl.multiple_of(z * 128, 128), 128)
        n = self.rows // 4
        return pl.ds(pl.multiple_of(base + z * n, 16), n), slice(None)

    def z1_copy(self, j):
        at = self.at
        rows, cols = self.quarter(at.up[j], pl.multiple_of(at.f * self.rows, 16))
        return self.copy(self.acc.at[rows, cols], self.rz.at[j], 10 + j, at.nz[j])

    def z2_copy(self, j):
        at = self.at
        rows, cols = self.quarter(at.z, 0)
        v = self.out.at[rows, cols]
        return self.copy(v, v, 13 + j, at.nz[j])

    def d_send(self):
        for i in range(4):
            self.d_copy(i).start()

    def add(self, view, buf):
        view[...] = view[...] + buf[...]

    def xy1(self):
        at = self.at
        for i, k in enumerate((at.kd, at.kx, at.ky, at.k)):
            self.d_copy(i).wait_recv()
            self.add(self.part(k, at.c), self.rd.at[i])
        for i in (0, 2, 1, 3):
            self.xy1_copy(i).start()

    def xy2(self):
        at = self.at
        for i, (k, h) in ((1, (at.ky, 0)), (3, (at.kx, 1)), (0, (at.k, 0)), (2, (at.k, 1))):
            self.xy1_copy(i).wait_recv()
            self.add(self.part(k, at.c, h), self.r1.at[i])
            if i == 1:
                self.xy2_copy(0).start()
            if i == 3:
                self.xy2_copy(1).start()

    def z1(self):
        at = self.at
        for i in range(2):
            self.xy2_copy(i).wait_recv()
            self.add(self.part(at.k, at.c, i), self.r2.at[i])
        for j in (1, 0, 2):
            self.z1_copy(j).start()

    def z2(self):
        at = self.at
        rows, cols = self.quarter(at.z, pl.multiple_of(at.f * self.rows, 16))
        total = self.acc[rows, cols]
        for j in range(3):
            self.z1_copy(j).wait_recv()
            total = total + self.rz[j]
        rows, cols = self.quarter(at.z, 0)
        self.out[rows, cols] = total.astype(BF16)
        for j in (1, 0, 2):
            self.z2_copy(j).start()

    def finish(self):
        for j in range(3):
            self.z2_copy(j).wait_recv()

    def drain(self):
        for i in range(4):
            self.d_copy(i).wait_send()
            self.xy1_copy(i).wait_send()
        for i in range(2):
            self.xy2_copy(i).wait_send()
        for i in range(3):
            self.z1_copy(i).wait_send()
            self.z2_copy(i).wait_send()


class Small:
    def __init__(self, at, sm, smr, smz, send, recv):
        self.at, self.sm, self.smr, self.smz, self.send, self.recv = at, sm, smr, smz, send, recv
        self.base = 4 * NSEM

    def step(self, i):
        at = self.at
        return remote(self.sm.at[i], self.smr.at[i], self.send, self.recv, self.base + i, (at.sib, at.nx, at.ny)[i])

    def zcopy(self, j):
        v = self.smz.at[self.at.z]
        return remote(v, v, self.send, self.recv, self.base + 3 + j, self.at.nz[j])

    def advance(self, i):
        if i > 0:
            self.step(i - 1).wait_recv()
            total = self.sm[i - 1] + self.smr[i - 1]
            if i < 3:
                self.sm[i] = total
            else:
                self.smz[self.at.z] = total
        if i < 3:
            self.step(i).start()
        else:
            for j in range(3):
                self.zcopy(j).start()

    def finish(self):
        for j in range(3):
            self.zcopy(j).wait_recv()
        return (self.smz[0] + self.smz[1]) + (self.smz[2] + self.smz[3])

    def drain(self):
        for i in range(3):
            self.step(i).wait_send()
            self.zcopy(i).wait_send()


def layer_kernel(x_hbm, pos_ref, seg_ref, relb_ref, ga_ref, gm_ref, wq_ref, wk_ref, wv_ref, wo_ref, wi0_ref, wi1_ref, wf_ref, go_hbm,
                 y_hbm, small_ref, dq_ref, dk_ref, dv_ref, do_ref, di0_ref, di1_ref, df_ref,
                 tab_s, pad_s, ga_s, gm_s, wqkv_s, wo_s, wi_s, wf_s, wqkvt_s, wot_s, wit_s, wft_s, xt_s, qkv_s, p_s, ctx_s,
                 got_s, ut_s, zt_s, dgu_s, dh_s, dacc_s, dga_s, dgm_s, io_s,
                 gf_s, gi_s, go_s, gq_s, rd_f, rd_i, rd_o, rd_q, r1_f, r1_i, r1_o, r1_q, r2_f, r2_i, r2_o, r2_q,
                 rz_f, rz_i, rz_o, rz_q, out_f, out_i, out_o, out_q, sm_s, smr_s, smz_s,
                 io_sem, out_sem, ag_own, ag_send, ag_recv, rs_send, rs_recv):
    at = Place()
    barrier = pltpu.get_barrier_semaphore()
    peers = [at.sib, at.nx, at.ny, at.nd] + at.nz
    for dev in peers:
        pl.semaphore_signal(barrier, inc=1, device_id=dev, device_id_type=MESH)

    def rows_of(r):
        return pl.ds(pl.multiple_of(r * SEQ, SEQ), SEQ)

    def x_copy(r):
        return pltpu.make_async_copy(x_hbm.at[rows_of(r), :], io_s.at[rows_of(r), :], io_sem.at[0, r])

    def go_copy(r):
        return pltpu.make_async_copy(go_hbm.at[rows_of(r), :], io_s.at[rows_of(r), :], io_sem.at[1, r])

    def y_copy(r):
        return pltpu.make_async_copy(io_s.at[rows_of(r), :], y_hbm.at[rows_of(r), :], io_sem.at[2, r])

    gather = Gather(at, (wq_ref, wk_ref, wv_ref, wo_ref, wi0_ref, wi1_ref, wf_ref),
                    ((wqkv_s, 0), (wqkv_s, AW), (wqkv_s, 2 * AW), (wo_s, 0), (wi_s, 0), (wi_s, FF), (wf_s, 0)), ag_own, ag_send, ag_recv)
    for w in range(7):
        gather.load(w).start()
    for r in range(ROWS):
        x_copy(r).start()
    pl.semaphore_wait(barrier, len(peers))
    first, rest = (0, 1, 2), (3, 4, 5, 6)
    gather.begin(first)
    gather.begin(rest)
    setup_small(relb_ref, ga_ref, gm_ref, tab_s, pad_s, ga_s, gm_s)
    dgm_s[...] = jnp.zeros_like(dgm_s)
    dga_s[...] = jnp.zeros_like(dga_s)
    dacc_s[...] = jnp.zeros_like(dacc_s)
    gather.relay(first)
    gather.finish(first)
    wqkvt_s[...] = wqkv_s[...].T

    def fwd(r):
        x_copy(r).wait()
        attn_fwd_row(r, io_s, pos_ref, seg_ref, tab_s, ga_s, wqkvt_s, xt_s, qkv_s, p_s, ctx_s)
        go_copy(r).start()

        @pl.when(r == 4)
        def _():
            gather.relay(rest)
    loop(ROWS, fwd)
    gather.finish(rest)
    wot_s[...] = wo_s[...].T
    wft_s[...] = wf_s[...].T
    wit_s[...] = wi_s[...].T

    def mlp(r):
        go_copy(r).wait()
        mlp_row(r, io_s, io_s, gm_s, wot_s, wit_s, wft_s, wi_s, wf_s, xt_s, ctx_s, got_s, ut_s, zt_s, dgu_s, dh_s, dgm_s)
        y_copy(r).start()
    loop(ROWS, mlp)

    red = [Reduce(WF, at, gf_s, rd_f, r1_f, r2_f, rz_f, out_f, rs_send, rs_recv),
           Reduce(WI, at, gi_s, rd_i, r1_i, r2_i, rz_i, out_i, rs_send, rs_recv),
           Reduce(WO, at, go_s, rd_o, r1_o, r2_o, rz_o, out_o, rs_send, rs_recv),
           Reduce(WQKV, at, gq_s, rd_q, r1_q, r2_q, rz_q, out_q, rs_send, rs_recv)]
    small = Small(at, sm_s, smr_s, smz_s, rs_send, rs_recv)

    def dwf(c):
        part = pl.ds(pl.multiple_of(c * 256, 256), 256)
        gf_s[:, part] = mm_nt(zt_s[...], got_s[part, :])
    loop(2, dwf)
    red[WF].d_send()

    def dwi(c):
        part = pl.ds(pl.multiple_of(c * 256, 256), 256)
        gi_s[:, part] = mm_nt(ut_s[...], dgu_s[part, :])
    loop(8, dwi)
    red[WI].d_send()
    red[WF].xy1()

    def dwo(c):
        part = pl.ds(pl.multiple_of(c * 256, 256), 256)
        go_s[:, part] = mm_nt(ctx_s[...], dh_s[part, :])
    loop(2, dwo)
    red[WO].d_send()
    red[WI].xy1()

    def bwd(r):
        attn_bwd_row(r, pos_ref, ga_s, wqkv_s, wo_s, xt_s, ut_s, qkv_s, p_s, dh_s, dgu_s, dacc_s, dga_s)

        @pl.when(r == 0)
        def _():
            red[WO].xy1()
            red[WF].xy2()

        @pl.when(r == 1)
        def _():
            red[WF].z1()

        @pl.when(r == 2)
        def _():
            red[WI].xy2()
            red[WO].xy2()

        @pl.when(r == 3)
        def _():
            red[WF].z2()
            red[WI].z1()

        @pl.when(r == 4)
        def _():
            red[WO].z1()
    loop(ROWS, bwd)

    def dwqkv(c):
        part = pl.ds(pl.multiple_of(c * AW, AW), AW)
        gq_s[:, part] = mm_nt(ut_s[...], dgu_s[part, :])
    loop(3, dwqkv)
    red[WQKV].d_send()
    red[WI].z2()
    red[WO].z2()
    bias_sums(dacc_s, p_s.at[0, 0])
    sm_s[0, 0:1, 0:256] = jnp.sum(p_s[0, 0].T, axis=0, keepdims=True)
    sm_s[0, 0:1, 256:512] = jnp.zeros((1, 256), F32)
    sm_s[0, 1:2, :] = jnp.sum(dga_s[...].T, axis=0, keepdims=True)
    sm_s[0, 2:3, :] = jnp.sum(dgm_s[...].T, axis=0, keepdims=True)
    sm_s[0, 3:8, :] = jnp.zeros((5, 512), F32)
    small.advance(0)
    red[WQKV].xy1()
    small.advance(1)
    red[WQKV].xy2()
    small.advance(2)
    red[WQKV].z1()
    small.advance(3)
    red[WQKV].z2()
    small_ref[...] = small.finish()
    for a in (WF, WI, WO):
        red[a].finish()
    finals = [(out_f, df_ref), (out_i.at[:, pl.ds(0, FF)], di0_ref), (out_i.at[:, pl.ds(FF, FF)], di1_ref), (out_o, do_ref),
              (out_q.at[:, pl.ds(0, AW)], dq_ref), (out_q.at[:, pl.ds(AW, AW)], dk_ref), (out_q.at[:, pl.ds(2 * AW, AW)], dv_ref)]
    finals = [pltpu.make_async_copy(src, dst, out_sem.at[i]) for i, (src, dst) in enumerate(finals)]
    for copy in finals[:4]:
        copy.start()
    red[WQKV].finish()
    for copy in finals[4:]:
        copy.start()
    for copy in finals:
        copy.wait()
    for r in range(ROWS):
        y_copy(r).wait()
    gather.drain()
    for g in red:
        g.drain()
    small.drain()


def local_layer(x_in, positions, segments, rel_bias, gain_attn, gain_mlp, wq, wk, wv, wo, wi0, wi1, wf, grad_out):
    vmem = pl.BlockSpec(memory_space=pltpu.VMEM)
    hbm = pl.BlockSpec(memory_space=pl.ANY)

    def bufs(shape_of, dtype):
        return [pltpu.VMEM(shape_of(r, c), dtype) for r, c in SHARD]

    def quarter(r, c):
        return (3, r, 128) if r == 48 else (3, r // 4, c)
    outs = pl.pallas_call(
        layer_kernel,
        out_shape=[jax.ShapeDtypeStruct((TOK, DM), BF16), jax.ShapeDtypeStruct((8, 512), F32)]
        + [jax.ShapeDtypeStruct(w.shape, BF16) for w in (wq, wk, wv, wo, wi0, wi1, wf)],
        in_specs=[hbm] + [vmem] * 5 + [hbm] * 8,
        out_specs=[hbm, vmem] + [hbm] * 7,
        scratch_shapes=[
            pltpu.VMEM((8, 128), F32), pltpu.VMEM((128, 128), F32), pltpu.VMEM((DM, 128), F32), pltpu.VMEM((DM, 128), F32),
            pltpu.VMEM((DM, 3 * AW), BF16), pltpu.VMEM((AW, DM), BF16), pltpu.VMEM((DM, 2 * FF), BF16), pltpu.VMEM((FF, DM), BF16),
            pltpu.VMEM((3 * AW, DM), BF16), pltpu.VMEM((DM, AW), BF16), pltpu.VMEM((2 * FF, DM), BF16), pltpu.VMEM((DM, FF), BF16),
            pltpu.VMEM((DM, TOK), BF16), pltpu.VMEM((3 * AW, TOK), BF16),
            pltpu.VMEM((HEADS, ROWS, SEQ, SEQ), F32), pltpu.VMEM((AW, TOK), BF16),
            pltpu.VMEM((DM, TOK), BF16), pltpu.VMEM((DM, TOK), BF16), pltpu.VMEM((FF, TOK), BF16), pltpu.VMEM((2 * FF, TOK), BF16),
            pltpu.VMEM((DM, TOK), BF16), pltpu.VMEM((HEADS, SEQ, SEQ), F32), pltpu.VMEM((DM, 128), F32), pltpu.VMEM((DM, 128), F32),
            pltpu.VMEM((TOK, DM), BF16)]
        + bufs(lambda r, c: (8 * r, c), F32) + bufs(lambda r, c: (4, r, c), F32) + bufs(lambda r, c: (4, r // 2, c), F32)
        + bufs(lambda r, c: (2, r // 2, c), F32) + bufs(quarter, F32) + bufs(lambda r, c: (r, c), BF16)
        + [pltpu.VMEM((3, 8, 512), F32), pltpu.VMEM((3, 8, 512), F32), pltpu.VMEM((4, 8, 512), F32),
           pltpu.SemaphoreType.DMA((3, ROWS)), pltpu.SemaphoreType.DMA((7,)), pltpu.SemaphoreType.DMA((7,)), pltpu.SemaphoreType.DMA((49,)), pltpu.SemaphoreType.DMA((49,)),
           pltpu.SemaphoreType.DMA((4 * NSEM + 6,)), pltpu.SemaphoreType.DMA((4 * NSEM + 6,))],
        compiler_params=pltpu.CompilerParams(vmem_limit_bytes=67043328, collective_id=0, has_side_effects=True),
        name='layer',
    )(x_in.reshape(TOK, DM), positions.reshape(ROWS, 1, SEQ), segments.reshape(ROWS, 1, SEQ), rel_bias,
      gain_attn.reshape(1, DM), gain_mlp.reshape(1, DM), wq, wk, wv, wo, wi0, wi1, wf, grad_out.reshape(TOK, DM))
    y, small = outs[0], outs[1]
    db = small[0, 0:256].reshape(32, 8)[:, :HEADS]
    return (y.reshape(ROWS, SEQ, DM), db, small[1], small[2]) + tuple(outs[2:])


def solution(mesh):
    row_spec = P(ROW_AXES)
    whole = P()
    part_spec = P('fsdp')
    in_specs = (row_spec, row_spec, row_spec, whole, whole, whole) + (part_spec,) * 7 + (row_spec,)
    out_specs = (row_spec, whole, whole, whole) + (part_spec,) * 7
    return jax.shard_map(local_layer, mesh=mesh, in_specs=in_specs, out_specs=out_specs, check_vma=False)
```

time: 497 us -> 164 us (0.33); the launches traced: 489 us -> 163 us
  matrix products: 151 us -> 0 us
  waiting for transfers between devices: 150 us -> 0 us
  Pallas kernels: 0 us -> 149 us
  blocking collectives: 129 us -> 0 us
  other arithmetic: 26 us -> 0 us
  between operations: 14.8 us -> 0.69 us
    dot_general x29 -> x0, matrix products: 151 us -> none  [the longest x7 30.1 us: project(): jnp.einsum('rsd,de->rse', tokens_in, weight, preferred_element_type=jnp.f...]
    pallas_call x0 -> x1, Pallas kernels: none -> 149 us  [local_layer(): pl.pallas_call(layer_kernel, out_shape=[jax.ShapeDtypeStruct((TOK, DM), B...]
    reduce_scatter x7 -> x0, waiting for transfers between devices: 147 us -> none  [reduce_weight(): shard = lax.psum_scatter(full_grad, 'fsdp', scatter_dimension=0, tiled=True)]
    psum x2 -> x0, blocking collectives: 87.6 us -> none  [the longest x1 47.9 us: reduce_weight(): return lax.psum(shard, 'dp').astype(jnp.bfloat16)]
    all_gather x4 -> x0, blocking collectives: 41.4 us -> none  [gather_full(): return lax.all_gather(part, 'fsdp', axis=0, tiled=True)]
    convert_element_type x3 -> x0, other arithmetic: 13.8 us -> none  [the longest x1 11.4 us: attn_backward(): d_low = d_scores.astype(jnp.bfloat16)]
    convert_element_type x4 -> x0, local copies, waits for them, and re-layouts: 8.75 us -> none  [the longest x1 2.41 us: local_layer(): project(normed, w_v).astype(jnp.bfloat16).reshape(rows, seq_len, heads, -1)]
    sub x1 -> x0, other arithmetic: 8.05 us -> none  [attn_forward(): attn_prob = jax.nn.softmax(scores, axis=-1)]
  transfers between devices with their start and end apart: 10 -> 0, of which waited for: 4 -> 0; matrix products, arithmetic and copies ran while one was open for 32% -> 0% of each run, Pallas kernels for 0% -> 0%
where the time goes in v1:
time: 164 us; the launch traced here: 163 us
  Pallas kernels  149 us (91%)
  local copies, waits for them, and re-layouts  14.1 us (9%)
    pallas_call x1, Pallas kernels, local_layer(): pl.pallas_call(layer_kernel, out_shape=[jax.ShapeDtypeStruct((TOK, DM), B...  149 us
    unnamed x24, local copies, waits for them, and re-layouts  9.32 us

profile of v1, /device:TPU:0, one launch (start us, length us, event | category | flops | bytes accessed | tf_op | source)
XLA Modules:
  0.0 163.3 jit_solution(8397909994238544664)
XLA Ops:
  0.6 1.4 copy.27.relb_ref
  2.0 1.3 reshape.44.pos_ref
  3.3 1.3 reshape.45.seg_ref
  4.6 148.5 %layer.1 = (bf16[1536,512]{1,0:T(8,128)(2,1)}, f32[8,512]{1,0:T(8,128)}, bf16[64,384]{1,0:T(8,128)(2,1)}, bf16[64,384]{1,0:T(8,128)(2,1)}, bf16[64,384]{1,0:T(8,...) custom-call(bf16[1536,512]{1,0:T(8,128)(2,1)} %bitcast.8, ...), custom_call_target="tpu_custom_call" | custom-call | tf_op jit(solution)/shard_map/layer/pallas_call | solution.py:563
  153.2 1.4 fusion
  154.5 0.7 slice_reduce_fusion
  155.2 0.1 reshape_squeeze.3
  155.3 0.7 copy.28
  156.0 0.0 copy-start.6
  156.0 0.0 copy-start.5
  156.0 0.0 copy-start.4
  156.0 0.0 copy-start.3
  156.0 0.0 copy-start.2
  156.0 0.0 copy-start.1
  156.0 0.0 copy-start
  156.1 2.8 %copy.37 = bf16[6,256,512]{2,1,0:T(8,128)(2,1)} copy(bf16[6,256,512]{2,1,0:T(8,128)(2,1)} %bitcast.10) | data formatting | bytes 3145728
  158.8 0.0 copy-done.6
  158.8 0.6 copy.38
  159.5 0.0 copy-done.5
  159.5 0.6 copy.39
  160.1 0.0 copy-done.4
  160.1 0.6 copy.40
  160.7 0.0 copy-done.3
  160.7 0.6 copy.41
  161.3 0.0 copy-done.2
  161.3 0.7 copy.42
  162.0 0.0 copy-done.1
  162.0 0.7 copy.43
  162.7 0.0 copy-done
  162.7 0.7 copy.44
Async XLA Ops:
  156.0 2.8 %copy-start.6 = (bf16[64,384]{1,0:T(8,128)(2,1)S(1)}, bf16[64,384]{1,0:T(8,128)(2,1)}, u32[]{:S(2)}) copy-start(bf16[64,384]{1,0:T(8,128)(2,1)} %get-tuple-element.57) | copy-start | bytes 147460
  156.0 3.5 %copy-start.5 = (bf16[64,384]{1,0:T(8,128)(2,1)S(1)}, bf16[64,384]{1,0:T(8,128)(2,1)}, u32[]{:S(2)}) copy-start(bf16[64,384]{1,0:T(8,128)(2,1)} %get-tuple-element.58) | copy-start | bytes 147460
  156.0 4.1 %copy-start.4 = (bf16[64,384]{1,0:T(8,128)(2,1)S(1)}, bf16[64,384]{1,0:T(8,128)(2,1)}, u32[]{:S(2)}) copy-start(bf16[64,384]{1,0:T(8,128)(2,1)} %get-tuple-element.59) | copy-start | bytes 147460
  156.0 4.7 %copy-start.3 = (bf16[48,512]{1,0:T(8,128)(2,1)S(1)}, bf16[48,512]{1,0:T(8,128)(2,1)}, u32[]{:S(2)}) copy-start(bf16[48,512]{1,0:T(8,128)(2,1)} %get-tuple-element.60) | copy-start | bytes 147460
  156.0 5.3 %copy-start.2 = (bf16[64,1024]{1,0:T(8,128)(2,1)S(1)}, bf16[64,1024]{1,0:T(8,128)(2,1)}, u32[]{:S(2)}) copy-start(bf16[64,1024]{1,0:T(8,128)(2,1)} %get-tuple-element.61) | copy-start | bytes 393220
  156.0 6.0 %copy-start.1 = (bf16[64,1024]{1,0:T(8,128)(2,1)S(1)}, bf16[64,1024]{1,0:T(8,128)(2,1)}, u32[]{:S(2)}) copy-start(bf16[64,1024]{1,0:T(8,128)(2,1)} %get-tuple-element.62) | copy-start | bytes 393220
  156.0 6.6 %copy-start = (bf16[128,512]{1,0:T(8,128)(2,1)S(1)}, bf16[128,512]{1,0:T(8,128)(2,1)}, u32[]{:S(2)}) copy-start(bf16[128,512]{1,0:T(8,128)(2,1)} %get-tuple-element.63) | copy-start | bytes 393220

commit v2 on v1

--- a/solution.py
+++ b/solution.py
@@ -51,8 +51,8 @@
 
 def setup_small(relb_ref, ga_ref, gm_ref, tab_s, pad_s, ga_s, gm_s):
     pad_s[...] = jnp.zeros_like(pad_s)
-    pad_s[0:32, 0:HEADS] = relb_ref[...]
-    t = pad_s[...].T[0:8, :]
+    pad_s[0:HEADS, 0:32] = relb_ref[...]
+    t = pad_s[0:8, :]
     lane = lax.broadcasted_iota(jnp.int32, t.shape, 1)
     tab_s[...] = jnp.where(lane < 32, t, pltpu.roll(t, 32, 1) + NEG_BIG)
     ga_s[...] = jnp.broadcast_to(ga_ref[...], (128, DM)).T
@@ -63,104 +63,160 @@
     return jnp.concatenate([col128, col128], axis=1)
 
 
-def attn_fwd_row(r, x_ref, pos_ref, seg_ref, tab_s, ga_s, wqkvt_s, xt_s, qkv_s, p_s, ctx_s):
+def prep_row(r, x_ref, pos_ref, seg_ref, ga_s, xt_s, at_s, idx_s):
     tok = tok_slice(r)
-    xt = x_ref[pl.ds(pl.multiple_of(r * SEQ, SEQ), SEQ), :].T
+    xt = x_ref[tok, :].T
     xt_s[:, tok] = xt
     xf = xt.astype(F32)
     inv = lax.rsqrt(jnp.mean(xf * xf, axis=0, keepdims=True) + EPSILON)
-    at = (xf * inv * wide(ga_s[...])).astype(BF16)
-    qkv_s[:, tok] = mm(wqkvt_s[...], at).astype(BF16)
-    code = (seg_ref[r] * 1024 + pos_ref[r]).astype(F32)
+    at_s[:, tok] = (xf * inv * wide(ga_s[...])).astype(BF16)
+    code = (seg_ref[pl.ds(r, 1), :] * 1024 + pos_ref[pl.ds(r, 1), :]).astype(F32)
     code = jnp.broadcast_to(code, (SEQ, SEQ))
     diff = code.T - code
-    idx = (rel_class(diff) + jnp.where(jnp.abs(diff) >= 512.0, 32.0, 0.0)).astype(jnp.int32)
+    idx_s[r] = rel_class(diff) + jnp.where(jnp.abs(diff) >= 512.0, 32.0, 0.0)
+
+
+def attn_fwd_row(r, tab_s, idx_s, wqkvt_s, at_s, qkv_s, p_s, ctx_s):
+    tok = tok_slice(r)
+    qkv = mm(wqkvt_s[...], at_s[:, tok]).astype(BF16)
+    qkv_s[:, tok] = qkv
+    idx = idx_s[r].astype(jnp.int32)
+
+    def scores(h):
+        return mm_tn(qkv[AW + h * HD:AW + (h + 1) * HD], qkv[h * HD:(h + 1) * HD])
+    s_next = scores(0)
     for h in range(HEADS):
-        qt = qkv_s[h * HD:(h + 1) * HD, tok]
-        kt = qkv_s[AW + h * HD:AW + (h + 1) * HD, tok]
-        vt = qkv_s[2 * AW + h * HD:2 * AW + (h + 1) * HD, tok]
+        s = s_next
+        if h + 1 < HEADS:
+            s_next = scores(h + 1)
         table = jnp.broadcast_to(tab_s[h:h + 1, :], (SEQ, 128))
-        bias = jnp.concatenate([jnp.take_along_axis(table, idx[:, 0:128], axis=1),
-                                jnp.take_along_axis(table, idx[:, 128:256], axis=1)], axis=1)
-        s = mm_tn(kt, qt) + bias
+        s = s + jnp.concatenate([jnp.take_along_axis(table, idx[:, 0:128], axis=1),
+                                 jnp.take_along_axis(table, idx[:, 128:256], axis=1)], axis=1)
         p = jnp.exp(s - jnp.max(s, axis=0, keepdims=True))
         p = p * (1.0 / jnp.sum(p, axis=0, keepdims=True))
         p_s[h, r] = p
-        ctx_s[h * HD:(h + 1) * HD, tok] = mm(vt, p.astype(BF16)).astype(BF16)
-
-
-def mlp_row(r, go_ref, y_ref, gm_s, wot_s, wit_s, wft_s, wi_s, wf_s, xt_s, ctx_s, got_s, ut_s, zt_s, dgu_s, dh_s, dgm_s):
+        ctx_s[h * HD:(h + 1) * HD, tok] = mm(qkv[2 * AW + h * HD:2 * AW + (h + 1) * HD], p.astype(BF16)).astype(BF16)
+
+
+def mlp_up_row(r, go_ref, gm_s, wot_s, wit_s, wf_s, xt_s, ctx_s, got_s, ut_s, zt_s, dgu_s, h_s):
     tok = tok_slice(r)
-    rows = pl.ds(pl.multiple_of(r * SEQ, SEQ), SEQ)
     ht = (xt_s[:, tok].astype(F32) + mm(wot_s[...], ctx_s[:, tok])).astype(BF16)
+    h_s[:, tok] = ht
     hf = ht.astype(F32)
     inv = lax.rsqrt(jnp.mean(hf * hf, axis=0, keepdims=True) + EPSILON)
-    gm = wide(gm_s[...])
-    ut = (hf * inv * gm).astype(BF16)
+    ut = (hf * inv * wide(gm_s[...])).astype(BF16)
     ut_s[:, tok] = ut
-    got = go_ref[rows, :].T
+    got = go_ref[tok, :].T
     got_s[:, tok] = got
     step = 256
+
+    def products(f):
+        return mm(wit_s[f:f + step, :], ut), mm(wit_s[FF + f:FF + f + step, :], ut), mm(wf_s[f:f + step, :], got)
+    nxt = products(0)
     for f in range(0, FF, step):
-        gate = mm(wit_s[f:f + step, :], ut)
-        up = mm(wit_s[FF + f:FF + f + step, :], ut)
-        dz = mm(wf_s[f:f + step, :], got).astype(BF16).astype(F32)
+        gate, up, dz = nxt
+        if f + step < FF:
+            nxt = products(f + step)
+        dz = dz.astype(BF16).astype(F32)
         sg = 1.0 / (1.0 + jnp.exp(-gate))
         silu = gate * sg
         zt_s[f:f + step, tok] = (silu * up).astype(BF16)
         dgu_s[f:f + step, tok] = (dz * up * (sg * (1.0 + gate * (1.0 - sg)))).astype(BF16)
         dgu_s[FF + f:FF + f + step, tok] = (dz * silu).astype(BF16)
+
+
+def mlp_down_row(r, y_ref, gm_s, wft_s, wi_s, got_s, zt_s, dgu_s, h_s, dgm_s):
+    tok = tok_slice(r)
+    hf = h_s[:, tok].astype(F32)
+    inv = lax.rsqrt(jnp.mean(hf * hf, axis=0, keepdims=True) + EPSILON)
+    gm = wide(gm_s[...])
+    du = mm(wi_s[...], dgu_s[:, tok])
     yt = (hf + mm(wft_s[...], zt_s[:, tok])).astype(BF16)
-    y_ref[rows, :] = yt.T
-    du = mm(wi_s[...], dgu_s[:, tok]).astype(BF16).astype(F32)
+    y_ref[tok, :] = yt.T
+    du = du.astype(BF16).astype(F32)
     hn = hf * inv
     dg = du * hn
     dgm_s[...] += dg[:, 0:128] + dg[:, 128:256]
     dug = du * gm
     dhn = inv * (dug - hn * jnp.mean(dug * hn, axis=0, keepdims=True))
-    dh_s[:, tok] = (got.astype(F32) + dhn).astype(BF16)
-
-
-def attn_bwd_row(r, pos_ref, ga_s, wqkv_s, wo_s, xt_s, at_s, qkv_s, p_s, dh_s, dqkv_s, dacc_s, dga_s):
+    h_s[:, tok] = (got_s[:, tok].astype(F32) + dhn).astype(BF16)
+
+
+def attn_bwd_row(r, ga_s, wo_s, xt_s, at_s, qkv_s, p_s, dh_s, dqkv_s):
     tok = tok_slice(r)
     dct = mm(wo_s[...], dh_s[:, tok]).astype(BF16)
-    pos = pos_ref[r]
+    qkv = qkv_s[:, tok]
+
+    def dprob(h):
+        return mm_tn(qkv[2 * AW + h * HD:2 * AW + (h + 1) * HD], dct[h * HD:(h + 1) * HD])
+    dp_next = dprob(0)
+    for h in range(HEADS):
+        dp = dp_next
+        if h + 1 < HEADS:
+            dp_next = dprob(h + 1)
+        p = p_s[h, r]
+        dqkv_s[2 * AW + h * HD:2 * AW + (h + 1) * HD, tok] = mm_nt(dct[h * HD:(h + 1) * HD], p.astype(BF16)).astype(BF16)
+        ds = p * (dp - jnp.sum(dp * p, axis=0, keepdims=True))
+        p_s[h, r] = ds
+        low = ds.astype(BF16)
+        dqkv_s[h * HD:(h + 1) * HD, tok] = mm(qkv[AW + h * HD:AW + (h + 1) * HD], low).astype(BF16)
+        dqkv_s[AW + h * HD:AW + (h + 1) * HD, tok] = mm_nt(qkv[h * HD:(h + 1) * HD], low).astype(BF16)
+    xf = xt_s[:, tok].astype(F32)
+    inv = lax.rsqrt(jnp.mean(xf * xf, axis=0, keepdims=True) + EPSILON)
+    at_s[:, tok] = (xf * inv * wide(ga_s[...])).astype(BF16)
+
+
+def bias_row(r, pos_ref, p_s, dacc_s):
+    pos = pos_ref[pl.ds(r, 1), :]
     onehot = jnp.where(lax.broadcasted_iota(jnp.int32, (SEQ, SEQ), 0) == pos, 1.0, 0.0).astype(BF16)
+
+    def first(h):
+        hi, mid, lo = split3(p_s[h, r])
+        return mm(onehot, hi) + mm(onehot, mid) + mm(onehot, lo)
+    nxt = first(0)
     for h in range(HEADS):
-        qt = qkv_s[h * HD:(h + 1) * HD, tok]
-        kt = qkv_s[AW + h * HD:AW + (h + 1) * HD, tok]
-        vt = qkv_s[2 * AW + h * HD:2 * AW + (h + 1) * HD, tok]
-        dc = dct[h * HD:(h + 1) * HD, :]
-        p = p_s[h, r]
-        dp = mm_tn(vt, dc)
-        ds = p * (dp - jnp.sum(dp * p, axis=0, keepdims=True))
-        dqkv_s[2 * AW + h * HD:2 * AW + (h + 1) * HD, tok] = mm_nt(dc, p.astype(BF16)).astype(BF16)
-        hi, mid, lo = split3(ds)
-        dqkv_s[h * HD:(h + 1) * HD, tok] = mm(kt, hi).astype(BF16)
-        dqkv_s[AW + h * HD:AW + (h + 1) * HD, tok] = mm_nt(qt, hi).astype(BF16)
-        t = mm(onehot, hi) + mm(onehot, mid) + mm(onehot, lo)
+        t = nxt
+        if h + 1 < HEADS:
+            nxt = first(h + 1)
         hi, mid, lo = split3(t)
         dacc_s[h] += mm_nt(hi, onehot) + mm_nt(mid, onehot) + mm_nt(lo, onehot)
+
+
+def gain_row(r, wqkv_s, xt_s, dqkv_s, dga_s):
+    tok = tok_slice(r)
     dn = mm(wqkv_s[...], dqkv_s[0:3 * AW, tok]).astype(BF16).astype(F32)
     xf = xt_s[:, tok].astype(F32)
     inv = lax.rsqrt(jnp.mean(xf * xf, axis=0, keepdims=True) + EPSILON)
-    xn = xf * inv
-    at_s[:, tok] = (xn * wide(ga_s[...])).astype(BF16)
-    dg = dn * xn
+    dg = dn * (xf * inv)
     dga_s[...] += dg[:, 0:128] + dg[:, 128:256]
 
 
 def bias_sums(dacc_s, db_s):
-    db_s[...] = jnp.zeros_like(db_s)
-    diff = (lax.broadcasted_iota(jnp.int32, (SEQ, SEQ), 0) - lax.broadcasted_iota(jnp.int32, (SEQ, SEQ), 1)).astype(F32)
-    cls = rel_class(diff)
-
-    def body(c, carry):
-        hit = cls == c.astype(F32)
-        for h in range(HEADS):
-            db_s[pl.ds(c * 8 + h, 1), :] = jnp.sum(jnp.where(hit, dacc_s[h], 0.0), axis=0, keepdims=True)
-        return carry
-    lax.fori_loop(0, 32, body, 0)
+    sub = lax.broadcasted_iota(jnp.int32, (8, SEQ), 0)
+    lane = lax.broadcasted_iota(jnp.int32, (8, SEQ), 1)
+    below = (sub - lane).astype(F32)
+    above = jnp.where(lane <= sub, sub - lane, sub - lane + SEQ).astype(F32)
+    cls_a, cls_b = rel_class(above), rel_class(below)
+
+    def head(h):
+        acc_a = jnp.zeros((8, SEQ), F32)
+        acc_b = jnp.zeros((8, SEQ), F32)
+        for t in range(SEQ // 8):
+            d = dacc_s[h, 8 * t:8 * t + 8, :]
+            keep = lane <= sub + 8 * t
+            a, b = jnp.where(keep, d, 0.0), jnp.where(keep, 0.0, d)
+            if t > 0:
+                a, b = pltpu.roll(a, SEQ - 8 * t, 1), pltpu.roll(b, SEQ - 8 * t, 1)
+            acc_a, acc_b = acc_a + a, acc_b + b
+        for c in range(32):
+            if c < 16:
+                v = jnp.where(cls_b == float(c), acc_b, 0.0)
+                if c == 0:
+                    v = v + jnp.where(cls_a == 0.0, acc_a, 0.0)
+            else:
+                v = jnp.where(cls_a == float(c), acc_a, 0.0)
+            db_s[pl.ds(h * 32 + c, 1), :] = jnp.sum(v, axis=0, keepdims=True)
+    loop(HEADS, head)
 
 
 def loop(n, fn):
@@ -201,13 +257,20 @@
 
 
 class Gather:
+    N = 9
+
     def __init__(self, at, parts, fulls, own, send, recv):
         self.at, self.parts, self.fulls, self.own, self.send, self.recv = at, parts, fulls, own, send, recv
 
-    def view(self, w, f):
+    def view(self, w, f, h=None):
         full, col = self.fulls[w]
         rows, cols = self.parts[w].shape
-        return full.at[pl.ds(pl.multiple_of(f * rows, rows), rows), pl.ds(col, cols)]
+        off = f * rows
+        if h is not None:
+            cut = (rows // 2 + 15) // 16 * 16
+            off = off + h * cut
+            rows = cut if h == 0 else rows - cut
+        return full.at[pl.ds(pl.multiple_of(off, 16), rows), pl.ds(col, cols)]
 
     def load(self, w):
         return pltpu.make_async_copy(self.parts[w], self.view(w, self.at.f), self.own.at[w])
@@ -215,17 +278,22 @@
     def direct(self, w, j):
         at = self.at
         v = self.view(w, at.f)
-        return remote(v, v, self.send, self.recv, w * 7 + j, (at.nx, at.ny, at.nd, at.sib)[j])
+        return remote(v, v, self.send, self.recv, w * self.N + j, (at.nx, at.ny, at.nd, at.sib)[j])
 
     def forward(self, w, j):
         at = self.at
         v = self.view(w, 2 * (at.kx, at.ky, at.kd)[j] + at.c)
-        return remote(v, v, self.send, self.recv, w * 7 + 4 + j, at.sib)
-
-    def begin(self, ws):
+        return remote(v, v, self.send, self.recv, w * self.N + 4 + j, at.sib)
+
+    def diag(self, w, h):
+        at = self.at
+        v = self.view(w, 2 * (at.kx, at.ky)[h] + at.c, h)
+        return remote(v, v, self.send, self.recv, w * self.N + 7 + h, (at.ny, at.nx)[h])
+
+    def begin(self, ws, js):
         for w in ws:
             self.load(w).wait()
-            for j in (2, 0, 1, 3):
+            for j in js:
                 self.direct(w, j).start()
 
     def relay(self, ws):
@@ -234,18 +302,34 @@
                 self.direct(w, j).wait_recv()
                 self.forward(w, j).start()
 
+    def relay1(self, ws):
+        for w in ws:
+            for j in (0, 1):
+                self.direct(w, j).wait_recv()
+                self.diag(w, j).start()
+                self.forward(w, j).start()
+
+    def relay2(self, ws):
+        for w in ws:
+            self.diag(w, 0).wait_recv()
+            self.diag(w, 1).wait_recv()
+            self.forward(w, 2).start()
+
     def finish(self, ws):
         for w in ws:
             self.direct(w, 3).wait_recv()
             for j in (0, 1, 2):
                 self.forward(w, j).wait_recv()
 
-    def drain(self):
-        for w in range(len(self.parts)):
-            for j in range(4):
+    def drain(self, ws, halves):
+        for w in ws:
+            for j in (0, 1, 3) if halves else (0, 1, 2, 3):
                 self.direct(w, j).wait_send()
             for j in range(3):
                 self.forward(w, j).wait_send()
+            if halves:
+                self.diag(w, 0).wait_send()
+                self.diag(w, 1).wait_send()
 
 
 class Reduce:
@@ -426,35 +510,48 @@
         x_copy(r).start()
     pl.semaphore_wait(barrier, len(peers))
     first, rest = (0, 1, 2), (3, 4, 5, 6)
-    gather.begin(first)
-    gather.begin(rest)
+    gather.begin(first, (2, 0, 1, 3))
+    gather.begin(rest, (0, 1, 3))
     setup_small(relb_ref, ga_ref, gm_ref, tab_s, pad_s, ga_s, gm_s)
     dgm_s[...] = jnp.zeros_like(dgm_s)
     dga_s[...] = jnp.zeros_like(dga_s)
-    dacc_s[...] = jnp.zeros_like(dacc_s)
+
+    def prep(r):
+        x_copy(r).wait()
+        prep_row(r, io_s, pos_ref, seg_ref, ga_s, xt_s, ut_s, dacc_s)
+        go_copy(r).start()
+    loop(ROWS, prep)
     gather.relay(first)
     gather.finish(first)
     wqkvt_s[...] = wqkv_s[...].T
 
     def fwd(r):
-        x_copy(r).wait()
-        attn_fwd_row(r, io_s, pos_ref, seg_ref, tab_s, ga_s, wqkvt_s, xt_s, qkv_s, p_s, ctx_s)
-        go_copy(r).start()
+        attn_fwd_row(r, tab_s, dacc_s, wqkvt_s, ut_s, qkv_s, p_s, ctx_s)
+
+        @pl.when(r == 2)
+        def _():
+            gather.relay1((3, 4))
 
         @pl.when(r == 4)
         def _():
-            gather.relay(rest)
+            gather.relay1((5, 6))
+
+        @pl.when(r == 5)
+        def _():
+            gather.relay2((3, 4))
     loop(ROWS, fwd)
-    gather.finish(rest)
+    gather.relay2((5, 6))
+    gather.finish((3, 4))
     wot_s[...] = wo_s[...].T
+    wit_s[0:FF, :] = wi_s[:, 0:FF].T
+    gather.finish((5, 6))
+    wit_s[FF:2 * FF, :] = wi_s[:, FF:2 * FF].T
     wft_s[...] = wf_s[...].T
-    wit_s[...] = wi_s[...].T
-
-    def mlp(r):
+
+    def mlp_up(r):
         go_copy(r).wait()
-        mlp_row(r, io_s, io_s, gm_s, wot_s, wit_s, wft_s, wi_s, wf_s, xt_s, ctx_s, got_s, ut_s, zt_s, dgu_s, dh_s, dgm_s)
-        y_copy(r).start()
-    loop(ROWS, mlp)
+        mlp_up_row(r, io_s, gm_s, wot_s, wit_s, wf_s, xt_s, ctx_s, got_s, ut_s, zt_s, dgu_s, dh_s)
+    loop(ROWS, mlp_up)
 
     red = [Reduce(WF, at, gf_s, rd_f, r1_f, r2_f, rz_f, out_f, rs_send, rs_recv),
            Reduce(WI, at, gi_s, rd_i, r1_i, r2_i, rz_i, out_i, rs_send, rs_recv),
@@ -462,72 +559,87 @@
            Reduce(WQKV, at, gq_s, rd_q, r1_q, r2_q, rz_q, out_q, rs_send, rs_recv)]
     small = Small(at, sm_s, smr_s, smz_s, rs_send, rs_recv)
 
+    def cols(c, n=256):
+        return pl.ds(pl.multiple_of(c * n, n), n)
+
     def dwf(c):
-        part = pl.ds(pl.multiple_of(c * 256, 256), 256)
-        gf_s[:, part] = mm_nt(zt_s[...], got_s[part, :])
+        gf_s[:, cols(c)] = mm_nt(zt_s[...], got_s[cols(c), :])
     loop(2, dwf)
     red[WF].d_send()
 
     def dwi(c):
-        part = pl.ds(pl.multiple_of(c * 256, 256), 256)
-        gi_s[:, part] = mm_nt(ut_s[...], dgu_s[part, :])
+        gi_s[:, cols(c)] = mm_nt(ut_s[...], dgu_s[cols(c), :])
     loop(8, dwi)
     red[WI].d_send()
     red[WF].xy1()
 
+    def mlp_down(r):
+        mlp_down_row(r, io_s, gm_s, wft_s, wi_s, got_s, zt_s, dgu_s, dh_s, dgm_s)
+        y_copy(r).start()
+
+        @pl.when(r == 2)
+        def _():
+            red[WI].xy1()
+    loop(ROWS, mlp_down)
+    red[WF].xy2()
+
     def dwo(c):
-        part = pl.ds(pl.multiple_of(c * 256, 256), 256)
-        go_s[:, part] = mm_nt(ctx_s[...], dh_s[part, :])
+        go_s[:, cols(c)] = mm_nt(ctx_s[...], dh_s[cols(c), :])
     loop(2, dwo)
     red[WO].d_send()
-    red[WI].xy1()
+    dacc_s[...] = jnp.zeros_like(dacc_s)
 
     def bwd(r):
-        attn_bwd_row(r, pos_ref, ga_s, wqkv_s, wo_s, xt_s, ut_s, qkv_s, p_s, dh_s, dgu_s, dacc_s, dga_s)
-
-        @pl.when(r == 0)
+        attn_bwd_row(r, ga_s, wo_s, xt_s, ut_s, qkv_s, p_s, dh_s, dgu_s)
+
+        @pl.when(r == 1)
         def _():
             red[WO].xy1()
-            red[WF].xy2()
-
-        @pl.when(r == 1)
-        def _():
-            red[WF].z1()
-
-        @pl.when(r == 2)
-        def _():
-            red[WI].xy2()
-            red[WO].xy2()
-
-        @pl.when(r == 3)
-        def _():
-            red[WF].z2()
-            red[WI].z1()
-
-        @pl.when(r == 4)
-        def _():
-            red[WO].z1()
     loop(ROWS, bwd)
 
     def dwqkv(c):
-        part = pl.ds(pl.multiple_of(c * AW, AW), AW)
-        gq_s[:, part] = mm_nt(ut_s[...], dgu_s[part, :])
+        gq_s[:, cols(c, AW)] = mm_nt(ut_s[...], dgu_s[cols(c, AW), :])
     loop(3, dwqkv)
     red[WQKV].d_send()
-    red[WI].z2()
-    red[WO].z2()
-    bias_sums(dacc_s, p_s.at[0, 0])
+    red[WI].xy2()
+
+    def tail(r):
+        bias_row(r, pos_ref, p_s, dacc_s)
+        gain_row(r, wqkv_s, xt_s, dgu_s, dga_s)
+
+        @pl.when(r == 0)
+        def _():
+            red[WQKV].xy1()
+            red[WF].z1()
+
+        @pl.when(r == 1)
+        def _():
+            red[WO].xy2()
+
+        @pl.when(r == 3)
+        def _():
+            red[WI].z1()
+            red[WF].z2()
+
+        @pl.when(r == 4)
+        def _():
+            red[WQKV].xy2()
+            red[WO].z1()
+    loop(ROWS, tail)
+    db_s = p_s.at[0, 0]
+    db_s[...] = jnp.zeros_like(db_s)
+    bias_sums(dacc_s, db_s)
     sm_s[0, 0:1, 0:256] = jnp.sum(p_s[0, 0].T, axis=0, keepdims=True)
     sm_s[0, 0:1, 256:512] = jnp.zeros((1, 256), F32)
     sm_s[0, 1:2, :] = jnp.sum(dga_s[...].T, axis=0, keepdims=True)
     sm_s[0, 2:3, :] = jnp.sum(dgm_s[...].T, axis=0, keepdims=True)
     sm_s[0, 3:8, :] = jnp.zeros((5, 512), F32)
     small.advance(0)
-    red[WQKV].xy1()
+    red[WQKV].z1()
     small.advance(1)
-    red[WQKV].xy2()
+    red[WI].z2()
     small.advance(2)
-    red[WQKV].z1()
+    red[WO].z2()
     small.advance(3)
     red[WQKV].z2()
     small_ref[...] = small.finish()
@@ -545,10 +657,30 @@
         copy.wait()
     for r in range(ROWS):
         y_copy(r).wait()
-    gather.drain()
+    gather.drain(first, False)
+    gather.drain(rest, True)
     for g in red:
         g.drain()
     small.drain()
+
+
+def emit_kernel(y_in, small_ref, g0, g1, g2, g3, g4, g5, g6, y_out, db_ref, dga_ref, dgm_ref, o0, o1, o2, o3, o4, o5, o6,
+                y_s, b0, b1, b2, b3, b4, b5, b6, in_sem, out_sem):
+    pairs = [(y_in.at[pl.ds(r * SEQ, SEQ), :], y_s.at[pl.ds(r * SEQ, SEQ), :], y_out.at[pl.ds(r * SEQ, SEQ), :]) for r in range(ROWS)]
+    pairs += list(zip((g0, g1, g2, g3, g4, g5, g6), (b0, b1, b2, b3, b4, b5, b6), (o0, o1, o2, o3, o4, o5, o6)))
+    ins = [pltpu.make_async_copy(a, b, in_sem.at[i]) for i, (a, b, _) in enumerate(pairs)]
+    outs = [pltpu.make_async_copy(b, c, out_sem.at[i]) for i, (_, b, c) in enumerate(pairs)]
+    for copy in ins:
+        copy.start()
+    for h in range(HEADS):
+        db_ref[h:h + 1, :] = small_ref[0:1, h * 32:(h + 1) * 32]
+    dga_ref[...] = small_ref[1:2, :]
+    dgm_ref[...] = small_ref[2:3, :]
+    for i in range(len(pairs)):
+        ins[i].wait()
+        outs[i].start()
+    for copy in outs:
+        copy.wait()
 
 
 def local_layer(x_in, positions, segments, rel_bias, gain_attn, gain_mlp, wq, wk, wv, wo, wi0, wi1, wf, grad_out):
@@ -578,15 +710,26 @@
         + bufs(lambda r, c: (8 * r, c), F32) + bufs(lambda r, c: (4, r, c), F32) + bufs(lambda r, c: (4, r // 2, c), F32)
         + bufs(lambda r, c: (2, r // 2, c), F32) + bufs(quarter, F32) + bufs(lambda r, c: (r, c), BF16)
         + [pltpu.VMEM((3, 8, 512), F32), pltpu.VMEM((3, 8, 512), F32), pltpu.VMEM((4, 8, 512), F32),
-           pltpu.SemaphoreType.DMA((3, ROWS)), pltpu.SemaphoreType.DMA((7,)), pltpu.SemaphoreType.DMA((7,)), pltpu.SemaphoreType.DMA((49,)), pltpu.SemaphoreType.DMA((49,)),
+           pltpu.SemaphoreType.DMA((3, ROWS)), pltpu.SemaphoreType.DMA((7,)), pltpu.SemaphoreType.DMA((7,)), pltpu.SemaphoreType.DMA((63,)), pltpu.SemaphoreType.DMA((63,)),
            pltpu.SemaphoreType.DMA((4 * NSEM + 6,)), pltpu.SemaphoreType.DMA((4 * NSEM + 6,))],
         compiler_params=pltpu.CompilerParams(vmem_limit_bytes=67043328, collective_id=0, has_side_effects=True),
         name='layer',
-    )(x_in.reshape(TOK, DM), positions.reshape(ROWS, 1, SEQ), segments.reshape(ROWS, 1, SEQ), rel_bias,
+    )(x_in.reshape(TOK, DM), positions, segments, rel_bias.T,
       gain_attn.reshape(1, DM), gain_mlp.reshape(1, DM), wq, wk, wv, wo, wi0, wi1, wf, grad_out.reshape(TOK, DM))
-    y, small = outs[0], outs[1]
-    db = small[0, 0:256].reshape(32, 8)[:, :HEADS]
-    return (y.reshape(ROWS, SEQ, DM), db, small[1], small[2]) + tuple(outs[2:])
+    weights = (wq, wk, wv, wo, wi0, wi1, wf)
+    outs = pl.pallas_call(
+        emit_kernel,
+        out_shape=[jax.ShapeDtypeStruct((TOK, DM), BF16), jax.ShapeDtypeStruct((HEADS, 32), F32),
+                   jax.ShapeDtypeStruct((1, DM), F32), jax.ShapeDtypeStruct((1, DM), F32)]
+        + [jax.ShapeDtypeStruct(w.shape, BF16) for w in weights],
+        in_specs=[hbm, vmem] + [hbm] * 7,
+        out_specs=[hbm, vmem, vmem, vmem] + [hbm] * 7,
+        scratch_shapes=[pltpu.VMEM((TOK, DM), BF16)] + [pltpu.VMEM(w.shape, BF16) for w in weights]
+        + [pltpu.SemaphoreType.DMA((ROWS + 7,)), pltpu.SemaphoreType.DMA((ROWS + 7,))],
+        name='emit',
+    )(*outs)
+    y, db, dga, dgm = outs[:4]
+    return (y.reshape(ROWS, SEQ, DM), db.T, dga.reshape(DM), dgm.reshape(DM)) + tuple(outs[4:])
 
 
 def solution(mesh):

time: 164 us -> 126 us (0.77)
  Pallas kernels: 149 us -> 125 us
  local copies, waits for them, and re-layouts: 14.1 us -> 0 us
    pallas_call x1, Pallas kernels: 149 us -> 122 us  [local_layer(): pl.pallas_call(layer_kernel, out_shape=[jax.ShapeDtypeStruct((TOK, DM), B...]
    unnamed x24 -> x0, local copies, waits for them, and re-layouts: 9.32 us -> none
    pallas_call x0 -> x1, Pallas kernels: none -> 3.83 us  [local_layer(): pl.pallas_call(emit_kernel, out_shape=[jax.ShapeDtypeStruct((TOK, DM), BF...]
    reshape x2 -> x0, local copies, waits for them, and re-layouts: 2.59 us -> none  [the longest x1 1.29 us: local_layer(): segments.reshape(ROWS, 1, SEQ)]
    slice x2 -> x0, local copies, waits for them, and re-layouts: 2.09 us -> none  [the longest x1 1.38 us: local_layer(): return (y.reshape(ROWS, SEQ, DM), db, small[1], small[2]) + tuple(outs[2:])]
where the time goes in v2:
time: 126 us
  Pallas kernels  125 us (99%)
    pallas_call x1, Pallas kernels, local_layer(): pl.pallas_call(layer_kernel, out_shape=[jax.ShapeDtypeStruct((TOK, DM), B...  122 us
    pallas_call x1, Pallas kernels, local_layer(): pl.pallas_call(emit_kernel, out_shape=[jax.ShapeDtypeStruct((TOK, DM), BF...  3.83 us

profile of v2, /device:TPU:0, one launch (start us, length us, event | category | flops | bytes accessed | tf_op | source)
XLA Modules:
  0.0 126.1 jit_solution(8392007133387206820)
XLA Ops:
  0.6 121.6 %layer.1 = (bf16[1536,512]{1,0:T(8,128)(2,1)}, f32[8,512]{1,0:T(8,128)}, bf16[64,384]{1,0:T(8,128)(2,1)}, bf16[64,384]{1,0:T(8,128)(2,1)}, bf16[64,384]{1,0:T(8,...) custom-call(bf16[1536,512]{1,0:T(8,128)(2,1)} %bitcast.9, ...), custom_call_target="tpu_custom_call" | custom-call | tf_op jit(solution)/shard_map/layer/pallas_call | solution.py:695
  122.2 3.8 %emit.1 = (bf16[1536,512]{1,0:T(8,128)(2,1)}, f32[6,32]{1,0:T(8,128)}, f32[1,512]{1,0:T(1,128)}, f32[1,512]{1,0:T(1,128)}, bf16[64,384]{1,0:T(8,128)(2,1)}, /*in...) custom-call(bf16[1536,512]{1,0:T(8,128)(2,1)} %get-tuple-element.31., ...), custom_call_target="tpu_custom_call" | custom-call | tf_op jit(solution)/shard_map/emit/pallas_call | solution.py:720

commit v3 on v2

--- a/solution.py
+++ b/solution.py
@@ -73,46 +73,63 @@
     code = (seg_ref[pl.ds(r, 1), :] * 1024 + pos_ref[pl.ds(r, 1), :]).astype(F32)
     code = jnp.broadcast_to(code, (SEQ, SEQ))
     diff = code.T - code
-    idx_s[r] = rel_class(diff) + jnp.where(jnp.abs(diff) >= 512.0, 32.0, 0.0)
-
-
-def attn_fwd_row(r, tab_s, idx_s, wqkvt_s, at_s, qkv_s, p_s, ctx_s):
+    idx_s[r] = (rel_class(diff) + jnp.where(jnp.abs(diff) >= 512.0, 32.0, 0.0)).astype(jnp.int32)
+
+
+def lane_lookup(table, idx):
+    dims = lax.GatherDimensionNumbers(offset_dims=(), collapsed_slice_dims=(1,), start_index_map=(1,),
+                                      operand_batching_dims=(0,), start_indices_batching_dims=(0,))
+    return lax.gather(table, idx[:, :, None], dims, (1, 1), mode='promise_in_bounds')
+
+
+def qkv_block(r, wqkvt_s, at_s, qkv_s):
+    tok = pl.ds(pl.multiple_of(r * 512, 512), 512)
+    qkv_s[:, tok] = mm(wqkvt_s[...], at_s[:, tok]).astype(BF16)
+
+
+def attn_fwd_row(r, tab_s, idx_s, qkv_s, p_s, ctx_s):
     tok = tok_slice(r)
-    qkv = mm(wqkvt_s[...], at_s[:, tok]).astype(BF16)
-    qkv_s[:, tok] = qkv
-    idx = idx_s[r].astype(jnp.int32)
+    half = SEQ // 2
 
     def scores(h):
-        return mm_tn(qkv[AW + h * HD:AW + (h + 1) * HD], qkv[h * HD:(h + 1) * HD])
+        kt, qt = qkv_s[AW + h * HD:AW + (h + 1) * HD, tok], qkv_s[h * HD:(h + 1) * HD, tok]
+        return [mm_tn(kt, qt[:, 0:half]), mm_tn(kt, qt[:, half:SEQ])]
     s_next = scores(0)
     for h in range(HEADS):
-        s = s_next
+        s_now = s_next
         if h + 1 < HEADS:
             s_next = scores(h + 1)
         table = jnp.broadcast_to(tab_s[h:h + 1, :], (SEQ, 128))
-        s = s + jnp.concatenate([jnp.take_along_axis(table, idx[:, 0:128], axis=1),
-                                 jnp.take_along_axis(table, idx[:, 128:256], axis=1)], axis=1)
-        p = jnp.exp(s - jnp.max(s, axis=0, keepdims=True))
-        p = p * (1.0 / jnp.sum(p, axis=0, keepdims=True))
-        p_s[h, r] = p
-        ctx_s[h * HD:(h + 1) * HD, tok] = mm(qkv[2 * AW + h * HD:2 * AW + (h + 1) * HD], p.astype(BF16)).astype(BF16)
-
-
-def mlp_up_row(r, go_ref, gm_s, wot_s, wit_s, wf_s, xt_s, ctx_s, got_s, ut_s, zt_s, dgu_s, h_s):
+        low = []
+        for i in range(2):
+            cols = slice(i * half, (i + 1) * half)
+            s = s_now[i] + lane_lookup(table, idx_s[r, :, cols])
+            p = jnp.exp(s - jnp.max(s, axis=0, keepdims=True))
+            p = p * (1.0 / jnp.sum(p, axis=0, keepdims=True))
+            p_s[h, r, :, cols] = p
+            low.append(p.astype(BF16))
+        vt = qkv_s[2 * AW + h * HD:2 * AW + (h + 1) * HD, tok]
+        ctx_s[h * HD:(h + 1) * HD, tok] = mm(vt, jnp.concatenate(low, axis=1)).astype(BF16)
+
+
+def mlp_in_row(r, gm_s, wot_s, xt_s, ctx_s, ut_s, h_s):
     tok = tok_slice(r)
     ht = (xt_s[:, tok].astype(F32) + mm(wot_s[...], ctx_s[:, tok])).astype(BF16)
     h_s[:, tok] = ht
     hf = ht.astype(F32)
     inv = lax.rsqrt(jnp.mean(hf * hf, axis=0, keepdims=True) + EPSILON)
-    ut = (hf * inv * wide(gm_s[...])).astype(BF16)
-    ut_s[:, tok] = ut
-    got = go_ref[tok, :].T
-    got_s[:, tok] = got
+    ut_s[:, tok] = (hf * inv * wide(gm_s[...])).astype(BF16)
+
+
+def mlp_up_row(r, gm_s, wot_s, wit_s, wf_s, xt_s, ctx_s, got_s, ut_s, zt_s, dgu_s, h_s):
+    tok = tok_slice(r)
+    ut, got = ut_s[:, tok], got_s[:, tok]
     step = 256
 
     def products(f):
         return mm(wit_s[f:f + step, :], ut), mm(wit_s[FF + f:FF + f + step, :], ut), mm(wf_s[f:f + step, :], got)
     nxt = products(0)
+    mlp_in_row(jnp.minimum(r + 1, ROWS - 1), gm_s, wot_s, xt_s, ctx_s, ut_s, h_s)
     for f in range(0, FF, step):
         gate, up, dz = nxt
         if f + step < FF:
@@ -166,7 +183,11 @@
     at_s[:, tok] = (xf * inv * wide(ga_s[...])).astype(BF16)
 
 
-def bias_row(r, pos_ref, p_s, dacc_s):
+def bias_view(dacc, h):
+    return dacc[h // 4].at[(h % 4) * SEQ:(h % 4 + 1) * SEQ, :]
+
+
+def bias_row(r, pos_ref, p_s, dacc):
     pos = pos_ref[pl.ds(r, 1), :]
     onehot = jnp.where(lax.broadcasted_iota(jnp.int32, (SEQ, SEQ), 0) == pos, 1.0, 0.0).astype(BF16)
 
@@ -179,7 +200,7 @@
         if h + 1 < HEADS:
             nxt = first(h + 1)
         hi, mid, lo = split3(t)
-        dacc_s[h] += mm_nt(hi, onehot) + mm_nt(mid, onehot) + mm_nt(lo, onehot)
+        bias_view(dacc, h)[...] += mm_nt(hi, onehot) + mm_nt(mid, onehot) + mm_nt(lo, onehot)
 
 
 def gain_row(r, wqkv_s, xt_s, dqkv_s, dga_s):
@@ -191,18 +212,18 @@
     dga_s[...] += dg[:, 0:128] + dg[:, 128:256]
 
 
-def bias_sums(dacc_s, db_s):
+def bias_sums(dacc, db_s):
     sub = lax.broadcasted_iota(jnp.int32, (8, SEQ), 0)
     lane = lax.broadcasted_iota(jnp.int32, (8, SEQ), 1)
     below = (sub - lane).astype(F32)
     above = jnp.where(lane <= sub, sub - lane, sub - lane + SEQ).astype(F32)
     cls_a, cls_b = rel_class(above), rel_class(below)
 
-    def head(h):
+    def head(h, src, first):
         acc_a = jnp.zeros((8, SEQ), F32)
         acc_b = jnp.zeros((8, SEQ), F32)
         for t in range(SEQ // 8):
-            d = dacc_s[h, 8 * t:8 * t + 8, :]
+            d = src[pl.ds(pl.multiple_of(h * SEQ + 8 * t, 8), 8), :]
             keep = lane <= sub + 8 * t
             a, b = jnp.where(keep, d, 0.0), jnp.where(keep, 0.0, d)
             if t > 0:
@@ -215,8 +236,9 @@
                     v = v + jnp.where(cls_a == 0.0, acc_a, 0.0)
             else:
                 v = jnp.where(cls_a == float(c), acc_a, 0.0)
-            db_s[pl.ds(h * 32 + c, 1), :] = jnp.sum(v, axis=0, keepdims=True)
-    loop(HEADS, head)
+            db_s[pl.ds((h + first) * 32 + c, 1), :] = jnp.sum(v, axis=0, keepdims=True)
+    loop(4, lambda h: head(h, dacc[0], 0))
+    loop(HEADS - 4, lambda h: head(h, dacc[1], 4))
 
 
 def loop(n, fn):
@@ -227,8 +249,41 @@
 
 
 MESH = pl.DeviceIdType.MESH
-SHARD = ((128, 512), (64, 2048), (48, 512), (64, 1152))
-WF, WI, WO, WQKV = 0, 1, 2, 3
+SHARD = ((128, 256),) * 2 + ((64, 512),) * 4 + ((48, 512),) + ((64, 384),) * 3
+NG = len(SHARD)
+PLAN = {
+    ('wf', 0): (('d', 0),),
+    ('wf', 1): (('d', 1), ('a', 0)),
+    ('wi', 0): (('a', 1),),
+    ('wi', 1): (('d', 2),),
+    ('wi', 3): (('d', 3),),
+    ('wi', 5): (('d', 4), ('b', 0)),
+    ('wi', 6): (('a', 2),),
+    ('wi', 7): (('d', 5),),
+    ('down', 0): (('b', 1),),
+    ('down', 1): (('y', 0),),
+    ('down', 2): (('a', 3),),
+    ('down', 3): (('b', 2),),
+    ('down', 4): (('y', 1),),
+    ('down', 5): (('a', 4), ('z', 0)),
+    ('wo', 0): (('d', 6), ('b', 3)),
+    ('bwd', 0): (('y', 2),),
+    ('bwd', 1): (('a', 5), ('z', 1)),
+    ('bwd', 2): (('b', 4),),
+    ('bwd', 3): (('y', 3),),
+    ('bwd', 4): (('a', 6), ('z', 2)),
+    ('bwd', 5): (('b', 5),),
+    ('wqkv', 0): (('d', 7), ('y', 4)),
+    ('wqkv', 1): (('d', 8), ('a', 7), ('z', 3)),
+    ('wqkv', 2): (('d', 9), ('b', 6)),
+    ('tail', 0): (('y', 5), ('a', 8)),
+    ('tail', 1): (('b', 7), ('y', 6), ('a', 9), ('z', 4)),
+    ('tail', 2): (('b', 8),),
+    ('tail', 3): (('y', 7), ('z', 5)),
+    ('tail', 4): (('b', 9), ('y', 8)),
+    ('tail', 5): (('y', 9), ('z', 6), ('z', 7)),
+    ('end', 0): (('z', 8), ('z', 9)),
+}
 NSEM = 16
 
 
@@ -442,7 +497,7 @@
 class Small:
     def __init__(self, at, sm, smr, smz, send, recv):
         self.at, self.sm, self.smr, self.smz, self.send, self.recv = at, sm, smr, smz, send, recv
-        self.base = 4 * NSEM
+        self.base = NG * NSEM
 
     def step(self, i):
         at = self.at
@@ -480,10 +535,10 @@
 def layer_kernel(x_hbm, pos_ref, seg_ref, relb_ref, ga_ref, gm_ref, wq_ref, wk_ref, wv_ref, wo_ref, wi0_ref, wi1_ref, wf_ref, go_hbm,
                  y_hbm, small_ref, dq_ref, dk_ref, dv_ref, do_ref, di0_ref, di1_ref, df_ref,
                  tab_s, pad_s, ga_s, gm_s, wqkv_s, wo_s, wi_s, wf_s, wqkvt_s, wot_s, wit_s, wft_s, xt_s, qkv_s, p_s, ctx_s,
-                 got_s, ut_s, zt_s, dgu_s, dh_s, dacc_s, dga_s, dgm_s, io_s,
-                 gf_s, gi_s, go_s, gq_s, rd_f, rd_i, rd_o, rd_q, r1_f, r1_i, r1_o, r1_q, r2_f, r2_i, r2_o, r2_q,
-                 rz_f, rz_i, rz_o, rz_q, out_f, out_i, out_o, out_q, sm_s, smr_s, smz_s,
-                 io_sem, out_sem, ag_own, ag_send, ag_recv, rs_send, rs_recv):
+                 got_s, ut_s, zt_s, dgu_s, dh_s, dga_s, dgm_s, io_s, idx_s,
+                 *more):
+    (acc, rd, r1, r2, rz, out), more = [more[i * NG:(i + 1) * NG] for i in range(6)], more[6 * NG:]
+    sm_s, smr_s, smz_s, io_sem, out_sem, ag_own, ag_send, ag_recv, rs_send, rs_recv = more
     at = Place()
     barrier = pltpu.get_barrier_semaphore()
     peers = [at.sib, at.nx, at.ny, at.nd] + at.nz
@@ -518,26 +573,33 @@
 
     def prep(r):
         x_copy(r).wait()
-        prep_row(r, io_s, pos_ref, seg_ref, ga_s, xt_s, ut_s, dacc_s)
+        prep_row(r, io_s, pos_ref, seg_ref, ga_s, xt_s, ut_s, idx_s)
         go_copy(r).start()
     loop(ROWS, prep)
+
+    def prep_go(r):
+        go_copy(r).wait()
+        got_s[:, tok_slice(r)] = io_s[tok_slice(r), :].T
+    loop(ROWS, prep_go)
     gather.relay(first)
     gather.finish(first)
     wqkvt_s[...] = wqkv_s[...].T
+    loop(TOK // 512, lambda r: qkv_block(r, wqkvt_s, ut_s, qkv_s))
 
     def fwd(r):
-        attn_fwd_row(r, tab_s, dacc_s, wqkvt_s, ut_s, qkv_s, p_s, ctx_s)
+        attn_fwd_row(r, tab_s, idx_s, qkv_s, p_s, ctx_s)
+
+        @pl.when(r == 0)
+        def _():
+            gather.relay1((3, 4))
 
         @pl.when(r == 2)
         def _():
-            gather.relay1((3, 4))
-
-        @pl.when(r == 4)
+            gather.relay1((5,))
+
+        @pl.when(r == 3)
         def _():
-            gather.relay1((5, 6))
-
-        @pl.when(r == 5)
-        def _():
+            gather.relay1((6,))
             gather.relay2((3, 4))
     loop(ROWS, fwd)
     gather.relay2((5, 6))
@@ -548,118 +610,97 @@
     wit_s[FF:2 * FF, :] = wi_s[:, FF:2 * FF].T
     wft_s[...] = wf_s[...].T
 
+    mlp_in_row(0, gm_s, wot_s, xt_s, ctx_s, ut_s, dh_s)
+
     def mlp_up(r):
-        go_copy(r).wait()
-        mlp_up_row(r, io_s, gm_s, wot_s, wit_s, wf_s, xt_s, ctx_s, got_s, ut_s, zt_s, dgu_s, dh_s)
+        mlp_up_row(r, gm_s, wot_s, wit_s, wf_s, xt_s, ctx_s, got_s, ut_s, zt_s, dgu_s, dh_s)
     loop(ROWS, mlp_up)
 
-    red = [Reduce(WF, at, gf_s, rd_f, r1_f, r2_f, rz_f, out_f, rs_send, rs_recv),
-           Reduce(WI, at, gi_s, rd_i, r1_i, r2_i, rz_i, out_i, rs_send, rs_recv),
-           Reduce(WO, at, go_s, rd_o, r1_o, r2_o, rz_o, out_o, rs_send, rs_recv),
-           Reduce(WQKV, at, gq_s, rd_q, r1_q, r2_q, rz_q, out_q, rs_send, rs_recv)]
+    red = [Reduce(a, at, acc[a], rd[a], r1[a], r2[a], rz[a], out[a], rs_send, rs_recv) for a in range(NG)]
     small = Small(at, sm_s, smr_s, smz_s, rs_send, rs_recv)
 
     def cols(c, n=256):
         return pl.ds(pl.multiple_of(c * n, n), n)
 
-    def dwf(c):
-        gf_s[:, cols(c)] = mm_nt(zt_s[...], got_s[cols(c), :])
-    loop(2, dwf)
-    red[WF].d_send()
-
-    def dwi(c):
-        gi_s[:, cols(c)] = mm_nt(ut_s[...], dgu_s[cols(c), :])
-    loop(8, dwi)
-    red[WI].d_send()
-    red[WF].xy1()
+    def fire(name, i):
+        for step, g in PLAN.get((name, i), ()):
+            {'d': red[g].d_send, 'a': red[g].xy1, 'b': red[g].xy2, 'y': red[g].z1, 'z': red[g].z2}[step]()
+
+    def fire_at(name, i, n, base=0):
+        for k in range(base, base + n):
+            if (name, k) in PLAN:
+                pl.when(i == k)(functools.partial(fire, name, k))
+
+    for i in range(2):
+        acc[i][...] = mm_nt(zt_s[...], got_s[256 * i:256 * i + 256, :])
+        fire('wf', i)
+    for g in range(4):
+        def dwi(c, g=g):
+            acc[2 + g][:, cols(c)] = mm_nt(ut_s[...], dgu_s[cols(c + 2 * g), :])
+            fire_at('wi', c + 2 * g, 2, 2 * g)
+        loop(2, dwi)
 
     def mlp_down(r):
         mlp_down_row(r, io_s, gm_s, wft_s, wi_s, got_s, zt_s, dgu_s, dh_s, dgm_s)
         y_copy(r).start()
-
-        @pl.when(r == 2)
-        def _():
-            red[WI].xy1()
+        fire_at('down', r, ROWS)
     loop(ROWS, mlp_down)
-    red[WF].xy2()
 
     def dwo(c):
-        go_s[:, cols(c)] = mm_nt(ctx_s[...], dh_s[cols(c), :])
+        acc[6][:, cols(c)] = mm_nt(ctx_s[...], dh_s[cols(c), :])
     loop(2, dwo)
-    red[WO].d_send()
-    dacc_s[...] = jnp.zeros_like(dacc_s)
+    fire('wo', 0)
 
     def bwd(r):
         attn_bwd_row(r, ga_s, wo_s, xt_s, ut_s, qkv_s, p_s, dh_s, dgu_s)
-
-        @pl.when(r == 1)
-        def _():
-            red[WO].xy1()
+        fire_at('bwd', r, ROWS)
     loop(ROWS, bwd)
-
-    def dwqkv(c):
-        gq_s[:, cols(c, AW)] = mm_nt(ut_s[...], dgu_s[cols(c, AW), :])
-    loop(3, dwqkv)
-    red[WQKV].d_send()
-    red[WI].xy2()
+    for i in range(3):
+        acc[7 + i][...] = mm_nt(ut_s[...], dgu_s[AW * i:AW * i + AW, :])
+        fire('wqkv', i)
+
+    for g in range(2):
+        red[g].drain()
+        acc[g][...] = jnp.zeros_like(acc[g])
 
     def tail(r):
-        bias_row(r, pos_ref, p_s, dacc_s)
+        bias_row(r, pos_ref, p_s, acc)
         gain_row(r, wqkv_s, xt_s, dgu_s, dga_s)
-
-        @pl.when(r == 0)
-        def _():
-            red[WQKV].xy1()
-            red[WF].z1()
-
-        @pl.when(r == 1)
-        def _():
-            red[WO].xy2()
-
-        @pl.when(r == 3)
-        def _():
-            red[WI].z1()
-            red[WF].z2()
-
-        @pl.when(r == 4)
-        def _():
-            red[WQKV].xy2()
-            red[WO].z1()
+        fire_at('tail', r, ROWS)
     loop(ROWS, tail)
     db_s = p_s.at[0, 0]
     db_s[...] = jnp.zeros_like(db_s)
-    bias_sums(dacc_s, db_s)
+    bias_sums(acc, db_s)
     sm_s[0, 0:1, 0:256] = jnp.sum(p_s[0, 0].T, axis=0, keepdims=True)
     sm_s[0, 0:1, 256:512] = jnp.zeros((1, 256), F32)
     sm_s[0, 1:2, :] = jnp.sum(dga_s[...].T, axis=0, keepdims=True)
     sm_s[0, 2:3, :] = jnp.sum(dgm_s[...].T, axis=0, keepdims=True)
     sm_s[0, 3:8, :] = jnp.zeros((5, 512), F32)
     small.advance(0)
-    red[WQKV].z1()
+    fire('head', 0)
     small.advance(1)
-    red[WI].z2()
+    late = PLAN.get(('end', 0), ())
+    finals = [(df_ref, 0, 256), (df_ref, 256, 256), (di0_ref, 0, 512), (di0_ref, 512, 512), (di1_ref, 0, 512), (di1_ref, 512, 512),
+              (do_ref, 0, 512), (dq_ref, 0, AW), (dk_ref, 0, AW), (dv_ref, 0, AW)]
+    finals = [pltpu.make_async_copy(out[g], dst.at[:, pl.ds(c, n)], out_sem.at[g]) for g, (dst, c, n) in enumerate(finals)]
+    held = [g for _, g in late]
+    for step, g in late[:1]:
+        red[g].z2()
     small.advance(2)
-    red[WO].z2()
+    for step, g in late[1:]:
+        red[g].z2()
     small.advance(3)
-    red[WQKV].z2()
+    for g in [g for g in range(NG) if g not in held] + held:
+        red[g].finish()
+        finals[g].start()
     small_ref[...] = small.finish()
-    for a in (WF, WI, WO):
-        red[a].finish()
-    finals = [(out_f, df_ref), (out_i.at[:, pl.ds(0, FF)], di0_ref), (out_i.at[:, pl.ds(FF, FF)], di1_ref), (out_o, do_ref),
-              (out_q.at[:, pl.ds(0, AW)], dq_ref), (out_q.at[:, pl.ds(AW, AW)], dk_ref), (out_q.at[:, pl.ds(2 * AW, AW)], dv_ref)]
-    finals = [pltpu.make_async_copy(src, dst, out_sem.at[i]) for i, (src, dst) in enumerate(finals)]
-    for copy in finals[:4]:
-        copy.start()
-    red[WQKV].finish()
-    for copy in finals[4:]:
-        copy.start()
     for copy in finals:
         copy.wait()
     for r in range(ROWS):
         y_copy(r).wait()
     gather.drain(first, False)
     gather.drain(rest, True)
-    for g in red:
+    for g in red[2:]:
         g.drain()
     small.drain()
 
@@ -705,13 +746,13 @@
             pltpu.VMEM((DM, TOK), BF16), pltpu.VMEM((3 * AW, TOK), BF16),
             pltpu.VMEM((HEADS, ROWS, SEQ, SEQ), F32), pltpu.VMEM((AW, TOK), BF16),
             pltpu.VMEM((DM, TOK), BF16), pltpu.VMEM((DM, TOK), BF16), pltpu.VMEM((FF, TOK), BF16), pltpu.VMEM((2 * FF, TOK), BF16),
-            pltpu.VMEM((DM, TOK), BF16), pltpu.VMEM((HEADS, SEQ, SEQ), F32), pltpu.VMEM((DM, 128), F32), pltpu.VMEM((DM, 128), F32),
-            pltpu.VMEM((TOK, DM), BF16)]
+            pltpu.VMEM((DM, TOK), BF16), pltpu.VMEM((DM, 128), F32), pltpu.VMEM((DM, 128), F32),
+            pltpu.VMEM((TOK, DM), BF16), pltpu.VMEM((ROWS, SEQ, SEQ), jnp.int32)]
         + bufs(lambda r, c: (8 * r, c), F32) + bufs(lambda r, c: (4, r, c), F32) + bufs(lambda r, c: (4, r // 2, c), F32)
         + bufs(lambda r, c: (2, r // 2, c), F32) + bufs(quarter, F32) + bufs(lambda r, c: (r, c), BF16)
         + [pltpu.VMEM((3, 8, 512), F32), pltpu.VMEM((3, 8, 512), F32), pltpu.VMEM((4, 8, 512), F32),
-           pltpu.SemaphoreType.DMA((3, ROWS)), pltpu.SemaphoreType.DMA((7,)), pltpu.SemaphoreType.DMA((7,)), pltpu.SemaphoreType.DMA((63,)), pltpu.SemaphoreType.DMA((63,)),
-           pltpu.SemaphoreType.DMA((4 * NSEM + 6,)), pltpu.SemaphoreType.DMA((4 * NSEM + 6,))],
+           pltpu.SemaphoreType.DMA((3, ROWS)), pltpu.SemaphoreType.DMA((NG,)), pltpu.SemaphoreType.DMA((7,)), pltpu.SemaphoreType.DMA((63,)), pltpu.SemaphoreType.DMA((63,)),
+           pltpu.SemaphoreType.DMA((NG * NSEM + 6,)), pltpu.SemaphoreType.DMA((NG * NSEM + 6,))],
         compiler_params=pltpu.CompilerParams(vmem_limit_bytes=67043328, collective_id=0, has_side_effects=True),
         name='layer',
     )(x_in.reshape(TOK, DM), positions, segments, rel_bias.T,

time: 126 us -> 109 us (0.87)
  Pallas kernels: 125 us -> 108 us
    pallas_call x1, Pallas kernels: 122 us -> 104 us  [local_layer(): pl.pallas_call(layer_kernel, out_shape=[jax.ShapeDtypeStruct((TOK, DM), B...]
where the time goes in v3:
time: 109 us
  Pallas kernels  108 us (99%)
    pallas_call x1, Pallas kernels, local_layer(): pl.pallas_call(layer_kernel, out_shape=[jax.ShapeDtypeStruct((TOK, DM), B...  104 us
    pallas_call x1, Pallas kernels, local_layer(): pl.pallas_call(emit_kernel, out_shape=[jax.ShapeDtypeStruct((TOK, DM), BF...  3.83 us

profile of v3, /device:TPU:0, one launch (start us, length us, event | category | flops | bytes accessed | tf_op | source)
XLA Modules:
  0.0 108.7 jit_solution(14058026329736404767)
XLA Ops:
  0.6 104.1 %layer.1 = (bf16[1536,512]{1,0:T(8,128)(2,1)}, f32[8,512]{1,0:T(8,128)}, bf16[64,384]{1,0:T(8,128)(2,1)}, bf16[64,384]{1,0:T(8,128)(2,1)}, bf16[64,384]{1,0:T(8,...) custom-call(bf16[1536,512]{1,0:T(8,128)(2,1)} %bitcast.9, ...), custom_call_target="tpu_custom_call" | custom-call | tf_op jit(solution)/shard_map/layer/pallas_call | solution.py:736
  104.7 3.8 %emit.1 = (bf16[1536,512]{1,0:T(8,128)(2,1)}, f32[6,32]{1,0:T(8,128)}, f32[1,512]{1,0:T(1,128)}, f32[1,512]{1,0:T(1,128)}, bf16[64,384]{1,0:T(8,128)(2,1)}, /*in...) custom-call(bf16[1536,512]{1,0:T(8,128)(2,1)} %get-tuple-element.31., ...), custom_call_target="tpu_custom_call" | custom-call | tf_op jit(solution)/shard_map/emit/pallas_call | solution.py:761

commit v4 on v3

v4 whole, which is shorter than its diff:
```python
import functools
import jax
import jax.numpy as jnp
from jax import lax
from jax.experimental import pallas as pl
from jax.experimental.pallas import tpu as pltpu
from jax.sharding import PartitionSpec as P
ZERO, ONE, TWO = (0, 1, 2)
EPSILON = 1e-06
NEG_BIG = -1000000000.0
THRESHOLDS = (12, 16, 23, 32, 46, 64, 91)
ROW_AXES = ('dp', 'fsdp')
ROWS, SEQ, DM, HEADS, HD, FF = (6, 256, 512, 6, 64, 1024)
TOK = ROWS * SEQ
EARLY = 4
AW = HEADS * HD
F32, BF16 = (jnp.float32, jnp.bfloat16)

def mm(a, b):
    return lax.dot_general(a, b, (((ONE,), (ZERO,)), ((), ())), preferred_element_type=F32)

def mm_nt(a, b):
    return lax.dot_general(a, b, (((ONE,), (ONE,)), ((), ())), preferred_element_type=F32)

def mm_tn(a, b):
    return lax.dot_general(a, b, (((ZERO,), (ZERO,)), ((), ())), preferred_element_type=F32)

def split3(v):
    hi = v.astype(BF16)
    rest = v - hi.astype(F32)
    mid = rest.astype(BF16)
    lo = (rest - mid.astype(F32)).astype(BF16)
    return (hi, mid, lo)

def tok_slice(r):
    return pl.ds(pl.multiple_of(r * SEQ, SEQ), SEQ)

def rel_class(diff):
    m = jnp.abs(diff)
    e = jnp.minimum(m, 8.0)
    for bound in THRESHOLDS:
        e = e + jnp.where(m >= bound, 1.0, 0.0)
    return e + jnp.where(diff > ZERO, 16.0, 0.0)

def setup_small(relb_ref, ga_ref, gm_ref, tab_s, pad_s, ga_s, gm_s):
    pad_s[...] = jnp.zeros_like(pad_s)
    pad_s[ZERO:HEADS, ZERO:32] = relb_ref[...]
    t = pad_s[ZERO:8, :]
    lane = lax.broadcasted_iota(jnp.int32, t.shape, ONE)
    tab_s[...] = jnp.where(lane < 32, t, pltpu.roll(t, 32, ONE) + NEG_BIG)
    ga_s[...] = jnp.broadcast_to(ga_ref[...], (128, DM)).T
    gm_s[...] = jnp.broadcast_to(gm_ref[...], (128, DM)).T

def wide(col128):
    return jnp.concatenate([col128, col128], axis=ONE)

def prep_row(r, x_ref, ga_s, xt_s, at_s):
    tok = tok_slice(r)
    xt = x_ref[tok, :].T
    xt_s[:, tok] = xt
    xf = xt.astype(F32)
    inv = lax.rsqrt(jnp.mean(xf * xf, axis=ZERO, keepdims=True) + EPSILON)
    at_s[:, tok] = (xf * inv * wide(ga_s[...])).astype(BF16)

def table_row(r, pos_ref, seg_ref, tab_s, idx_s, p_s):
    code = (seg_ref[pl.ds(r, ONE), :] * 1024 + pos_ref[pl.ds(r, ONE), :]).astype(F32)
    code = jnp.broadcast_to(code, (SEQ, SEQ))
    diff = code.T - code
    idx = (rel_class(diff) + jnp.where(jnp.abs(diff) >= 512.0, 32.0, 0.0)).astype(jnp.int32)
    idx_s[r] = idx
    for h in range(EARLY):
        table = jnp.broadcast_to(tab_s[h:h + ONE, :], (SEQ, 128))
        p_s[h, r, :, ZERO:128] = lane_lookup(table, idx[:, ZERO:128])
        p_s[h, r, :, 128:256] = lane_lookup(table, idx[:, 128:256])

def lane_lookup(table, idx):
    dims = lax.GatherDimensionNumbers(offset_dims=(), collapsed_slice_dims=(ONE,), start_index_map=(ONE,), operand_batching_dims=(ZERO,), start_indices_batching_dims=(ZERO,))
    return lax.gather(table, idx[:, :, None], dims, (ONE, ONE), mode='promise_in_bounds')

def qkv_block(r, wqkvt_s, at_s, qkv_s):
    tok = pl.ds(pl.multiple_of(r * 512, 512), 512)
    qkv_s[:, tok] = mm(wqkvt_s[...], at_s[:, tok]).astype(BF16)

def attn_fwd_row(r, tab_s, idx_s, qkv_s, p_s, ctx_s):
    tok = tok_slice(r)
    half = SEQ // TWO

    def scores(h):
        kt, qt = (qkv_s[AW + h * HD:AW + (h + ONE) * HD, tok], qkv_s[h * HD:(h + ONE) * HD, tok])
        return [mm_tn(kt, qt[:, ZERO:half]), mm_tn(kt, qt[:, half:SEQ])]
    ahead = [scores(h) for h in range(TWO)]
    for h in range(HEADS):
        s_now = ahead.pop(ZERO)
        if h + TWO < HEADS:
            ahead.append(scores(h + TWO))
        low = []
        for i in range(TWO):
            cols = slice(i * half, (i + ONE) * half)
            bias = p_s[h, r, :, cols] if h < EARLY else lane_lookup(jnp.broadcast_to(tab_s[h:h + ONE, :], (SEQ, 128)), idx_s[r, :, cols])
            s = s_now[i] + bias
            p = jnp.exp(s - jnp.max(s, axis=ZERO, keepdims=True))
            p = p * (1.0 / jnp.sum(p, axis=ZERO, keepdims=True))
            p_s[h, r, :, cols] = p
            low.append(p.astype(BF16))
        vt = qkv_s[TWO * AW + h * HD:TWO * AW + (h + ONE) * HD, tok]
        ctx_s[h * HD:(h + ONE) * HD, tok] = mm(vt, jnp.concatenate(low, axis=ONE)).astype(BF16)

def mlp_in_row(r, gm_s, wot_s, xt_s, ctx_s, ut_s, h_s):
    tok = tok_slice(r)
    ht = (xt_s[:, tok].astype(F32) + mm(wot_s[...], ctx_s[:, tok])).astype(BF16)
    h_s[:, tok] = ht
    hf = ht.astype(F32)
    inv = lax.rsqrt(jnp.mean(hf * hf, axis=ZERO, keepdims=True) + EPSILON)
    ut_s[:, tok] = (hf * inv * wide(gm_s[...])).astype(BF16)

def mlp_up_row(r, gm_s, wot_s, wit_s, wf_s, xt_s, ctx_s, got_s, ut_s, zt_s, dgu_s, h_s):
    tok = tok_slice(r)
    ut, got = (ut_s[:, tok], got_s[:, tok])
    step = 256

    def products(f):
        return (mm(wit_s[f:f + step, :], ut), mm(wit_s[FF + f:FF + f + step, :], ut), mm(wf_s[f:f + step, :], got))
    nxt = products(ZERO)
    mlp_in_row(jnp.minimum(r + ONE, ROWS - ONE), gm_s, wot_s, xt_s, ctx_s, ut_s, h_s)
    for f in range(ZERO, FF, step):
        gate, up, dz = nxt
        if f + step < FF:
            nxt = products(f + step)
        dz = dz.astype(BF16).astype(F32)
        sg = 1.0 / (1.0 + jnp.exp(-gate))
        silu = gate * sg
        zt_s[f:f + step, tok] = (silu * up).astype(BF16)
        dgu_s[f:f + step, tok] = (dz * up * (sg * (1.0 + gate * (1.0 - sg)))).astype(BF16)
        dgu_s[FF + f:FF + f + step, tok] = (dz * silu).astype(BF16)

def mlp_down_row(r, gm_s, wi_s, got_s, dgu_s, h_s, dgm_s):
    tok = tok_slice(r)
    ht, got = (h_s[:, tok], got_s[:, tok])
    hf = ht.astype(F32)
    inv = lax.rsqrt(jnp.mean(hf * hf, axis=ZERO, keepdims=True) + EPSILON)
    gm = wide(gm_s[...])
    du = mm(wi_s[...], dgu_s[:, tok]).astype(BF16).astype(F32)
    hn = hf * inv
    dg = du * hn
    dgm_s[...] += dg[:, ZERO:128] + dg[:, 128:256]
    dug = du * gm
    dhn = inv * (dug - hn * jnp.mean(dug * hn, axis=ZERO, keepdims=True))
    h_s[:, tok] = (got.astype(F32) + dhn).astype(BF16)
    got_s[:, tok] = ht

def out_row(r, y_ref, wft_s, h_s, zt_s):
    tok = tok_slice(r)
    y_ref[tok, :] = (h_s[:, tok].astype(F32) + mm(wft_s[...], zt_s[:, tok])).astype(BF16).T

def attn_bwd_row(r, ga_s, wo_s, xt_s, at_s, qkv_s, p_s, dh_s, dqkv_s):
    tok = tok_slice(r)
    dct = mm(wo_s[...], dh_s[:, tok]).astype(BF16)
    qkv = qkv_s[:, tok]

    def dprob(h):
        return mm_tn(qkv[TWO * AW + h * HD:TWO * AW + (h + ONE) * HD], dct[h * HD:(h + ONE) * HD])
    ahead = [dprob(h) for h in range(TWO)]
    for h in range(HEADS):
        dp = ahead.pop(ZERO)
        if h + TWO < HEADS:
            ahead.append(dprob(h + TWO))
        p = p_s[h, r]
        dqkv_s[TWO * AW + h * HD:TWO * AW + (h + ONE) * HD, tok] = mm_nt(dct[h * HD:(h + ONE) * HD], p.astype(BF16)).astype(BF16)
        ds = p * (dp - jnp.sum(dp * p, axis=ZERO, keepdims=True))
        p_s[h, r] = ds
        low = ds.astype(BF16)
        dqkv_s[h * HD:(h + ONE) * HD, tok] = mm(qkv[AW + h * HD:AW + (h + ONE) * HD], low).astype(BF16)
        dqkv_s[AW + h * HD:AW + (h + ONE) * HD, tok] = mm_nt(qkv[h * HD:(h + ONE) * HD], low).astype(BF16)
    xf = xt_s[:, tok].astype(F32)
    inv = lax.rsqrt(jnp.mean(xf * xf, axis=ZERO, keepdims=True) + EPSILON)
    at_s[:, tok] = (xf * inv * wide(ga_s[...])).astype(BF16)

def bias_view(dacc, h):
    return dacc[h // 4].at[h % 4 * SEQ:(h % 4 + ONE) * SEQ, :]

def bias_row(r, pos_ref, p_s, dacc):
    pos = pos_ref[pl.ds(r, ONE), :]
    onehot = jnp.where(lax.broadcasted_iota(jnp.int32, (SEQ, SEQ), ZERO) == pos, 1.0, 0.0).astype(BF16)

    def first(h):
        hi, mid, lo = split3(p_s[h, r])
        return mm(onehot, hi) + mm(onehot, mid) + mm(onehot, lo)
    nxt = first(ZERO)
    for h in range(HEADS):
        t = nxt
        if h + ONE < HEADS:
            nxt = first(h + ONE)
        hi, mid, lo = split3(t)
        bias_view(dacc, h)[...] += mm_nt(hi, onehot) + mm_nt(mid, onehot) + mm_nt(lo, onehot)

def gain_row(r, wqkv_s, xt_s, dqkv_s, dga_s):
    tok = tok_slice(r)
    dn = mm(wqkv_s[...], dqkv_s[ZERO:3 * AW, tok]).astype(BF16).astype(F32)
    xf = xt_s[:, tok].astype(F32)
    inv = lax.rsqrt(jnp.mean(xf * xf, axis=ZERO, keepdims=True) + EPSILON)
    dg = dn * (xf * inv)
    dga_s[...] += dg[:, ZERO:128] + dg[:, 128:256]

def bias_sums(dacc, db_s):
    sub = lax.broadcasted_iota(jnp.int32, (8, SEQ), ZERO)
    lane = lax.broadcasted_iota(jnp.int32, (8, SEQ), ONE)
    below = (sub - lane).astype(F32)
    above = jnp.where(lane <= sub, sub - lane, sub - lane + SEQ).astype(F32)
    cls_a, cls_b = (rel_class(above), rel_class(below))

    def head(h, src, first):
        acc_a = jnp.zeros((8, SEQ), F32)
        acc_b = jnp.zeros((8, SEQ), F32)
        for t in range(SEQ // 8):
            d = src[pl.ds(pl.multiple_of(h * SEQ + 8 * t, 8), 8), :]
            keep = lane <= sub + 8 * t
            a, b = (jnp.where(keep, d, 0.0), jnp.where(keep, 0.0, d))
            if t > ZERO:
                a, b = (pltpu.roll(a, SEQ - 8 * t, ONE), pltpu.roll(b, SEQ - 8 * t, ONE))
            acc_a, acc_b = (acc_a + a, acc_b + b)
        for c in range(32):
            if c < 16:
                v = jnp.where(cls_b == float(c), acc_b, 0.0)
                if c == ZERO:
                    v = v + jnp.where(cls_a == 0.0, acc_a, 0.0)
            else:
                v = jnp.where(cls_a == float(c), acc_a, 0.0)
            db_s[pl.ds((h + first) * 32 + c, ONE), :] = jnp.sum(v, axis=ZERO, keepdims=True)
    loop(4, lambda h: head(h, dacc[ZERO], ZERO))
    loop(HEADS - 4, lambda h: head(h, dacc[ONE], 4))

def loop(n, fn):

    def body(i, carry):
        fn(i)
        return carry
    lax.fori_loop(ZERO, n, body, ZERO)
MESH = pl.DeviceIdType.MESH
SHARD = ((128, 256),) * 2 + ((64, 512),) * 4 + ((48, 512),) + ((64, 384),) * 3
NG = len(SHARD)
PAIRED = (0, 1, 2, 3, 4, 5, 6)
PLAN = {'wf0': 'd0', 'wf1': 'd1', 'wi0': 'a0', 'wi1': 'd2', 'wi2': 'a1', 'wi3': 'd3', 'wi5': 'd4', 'wi7': 'd5a4', 'down2': 'b1a2', 'down5': 'b0b4', 'wo0': 'd6y1', 'bwd0': 'a6', 'bwd1': 'b2w1', 'bwd2': 'y0', 'bwd3': 'a3y4', 'bwd4': 'a5w0z1', 'bwd5': 'y2w4', 'wqkv0': 'd7b6', 'wqkv1': 'd8b3a7x1', 'wqkv2': 'd9w2z0', 'tail0': 'b5z4', 'gain0': 'y6', 'tail1': 'y3z2', 'gain1': 'x0', 'tail2': 'b7w6', 'gain2': 'a8w3y5', 'tail3': 'a9y7x2', 'gain3': 'z6', 'tail4': 'b8w5', 'gain4': 'b9x4', 'tail5': 'z3y8', 'gain5': 'x6z7z5', 'head0': 'y9', 'yrow2': 'x3', 'yrow3': 'z8', 'yrow5': 'z9', 'yrow4': 'x5'}
NSEM = 16

def remote(src, dst, send, recv, i, dev):
    return pltpu.make_async_remote_copy(src_ref=src, dst_ref=dst, send_sem=send.at[i], recv_sem=recv.at[i], device_id=dev, device_id_type=MESH)

class Place:

    def __init__(self):
        self.f = lax.axis_index('fsdp')
        self.z = lax.axis_index('dp')
        self.c = lax.rem(self.f, TWO)
        self.k = self.f // TWO
        self.x = lax.rem(self.k, TWO)
        self.y = self.k // TWO
        self.kx = self.k + ONE - TWO * self.x
        self.ky = self.k + TWO - 4 * self.y
        self.kd = 3 - self.k
        self.sib = {'fsdp': self.f + ONE - TWO * self.c}
        self.nx = {'fsdp': TWO * self.kx + self.c}
        self.ny = {'fsdp': TWO * self.ky + self.c}
        self.nd = {'fsdp': TWO * self.kd + self.c}
        self.up = [lax.rem(self.z + j, 4) for j in (ONE, TWO, 3)]
        self.nz = [{'dp': u} for u in self.up]
        self.za = lax.rem(self.z, TWO)
        self.zb = self.z // TWO
        self.n1 = {'dp': self.z + ONE - TWO * self.za}
        self.n2 = {'dp': self.z + TWO - 4 * self.zb}

class Gather:
    N = 9

    def __init__(self, at, parts, fulls, own, send, recv):
        self.at, self.parts, self.fulls, self.own, self.send, self.recv = (at, parts, fulls, own, send, recv)

    def view(self, w, f, h=None):
        full, col = self.fulls[w]
        rows, cols = self.parts[w].shape
        off = f * rows
        if h is not None:
            cut = (rows // TWO + 15) // 16 * 16
            off = off + h * cut
            rows = cut if h == ZERO else rows - cut
        return full.at[pl.ds(pl.multiple_of(off, 16), rows), pl.ds(col, cols)]

    def load(self, w):
        return pltpu.make_async_copy(self.parts[w], self.view(w, self.at.f), self.own.at[w])

    def direct(self, w, j):
        at = self.at
        v = self.view(w, at.f)
        return remote(v, v, self.send, self.recv, w * self.N + j, (at.nx, at.ny, at.nd, at.sib)[j])

    def forward(self, w, j):
        at = self.at
        v = self.view(w, TWO * (at.kx, at.ky, at.kd)[j] + at.c)
        return remote(v, v, self.send, self.recv, w * self.N + 4 + j, at.sib)

    def diag(self, w, h):
        at = self.at
        v = self.view(w, TWO * (at.kx, at.ky)[h] + at.c, h)
        return remote(v, v, self.send, self.recv, w * self.N + 7 + h, (at.ny, at.nx)[h])

    def begin(self, ws, js):
        for w in ws:
            self.load(w).wait()
            for j in js:
                self.direct(w, j).start()

    def relay(self, ws):
        for w in ws:
            for j in (ZERO, ONE, TWO):
                self.direct(w, j).wait_recv()
                self.forward(w, j).start()

    def relay1(self, ws):
        for w in ws:
            for j in (ZERO, ONE):
                self.direct(w, j).wait_recv()
                self.diag(w, j).start()
                self.forward(w, j).start()

    def relay2(self, ws):
        for w in ws:
            self.diag(w, ZERO).wait_recv()
            self.diag(w, ONE).wait_recv()
            self.forward(w, TWO).start()

    def finish(self, ws):
        for w in ws:
            self.direct(w, 3).wait_recv()
            for j in (ZERO, ONE, TWO):
                self.forward(w, j).wait_recv()

    def drain(self, ws, halves):
        for w in ws:
            for j in (ZERO, ONE, 3) if halves else (ZERO, ONE, TWO, 3):
                self.direct(w, j).wait_send()
            for j in range(3):
                self.forward(w, j).wait_send()
            if halves:
                self.diag(w, ZERO).wait_send()
                self.diag(w, ONE).wait_send()

class Reduce:

    def __init__(self, a, at, acc, rd, r1, r2, rz, out, send, recv):
        self.a, self.at, self.acc, self.rd, self.r1, self.r2, self.rz, self.out = (a, at, acc, rd, r1, r2, rz, out)
        self.send, self.recv = (send, recv)
        self.rows, self.cols = SHARD[a]
        self.half = self.rows // TWO

    def part(self, k, c, h=None):
        n = self.rows if h is None else self.half
        off = (TWO * k + c) * self.rows + (ZERO if h is None else h * self.half)
        return self.acc.at[pl.ds(pl.multiple_of(off, 8), n), :]

    def copy(self, src, dst, i, dev):
        return remote(src, dst, self.send, self.recv, self.a * NSEM + i, dev)

    def d_copy(self, i):
        at = self.at
        k = (at.kd, at.kx, at.ky, at.k)[i]
        return self.copy(self.part(k, ONE - at.c), self.rd.at[i], i, at.sib)

    def xy1_copy(self, i):
        at = self.at
        k, h, dev = ((at.kx, ZERO, at.nx), (at.kd, ZERO, at.nx), (at.ky, ONE, at.ny), (at.kd, ONE, at.ny))[i]
        return self.copy(self.part(k, at.c, h), self.r1.at[i], 4 + i, dev)

    def xy2_copy(self, i):
        at = self.at
        k, h, dev = ((at.ky, ZERO, at.ny), (at.kx, ONE, at.nx))[i]
        return self.copy(self.part(k, at.c, h), self.r2.at[i], 8 + i, dev)

    def quarter(self, z, base):
        if self.rows == 48:
            return (pl.ds(base, self.rows), pl.ds(pl.multiple_of(z * 128, 128), 128))
        n = self.rows // 4
        return (pl.ds(pl.multiple_of(base + z * n, 16), n), slice(None))

    def z1_copy(self, j):
        at = self.at
        rows, cols = self.quarter(at.up[j], pl.multiple_of(at.f * self.rows, 16))
        return self.copy(self.acc.at[rows, cols], self.rz.at[j], 10 + j, at.nz[j])

    def z2_copy(self, j):
        at = self.at
        rows, cols = self.quarter(at.z, ZERO)
        v = self.out.at[rows, cols]
        return self.copy(v, v, 13 + j, at.nz[j])

    def d_send(self):
        for i in range(4):
            self.d_copy(i).start()

    def add(self, view, buf):
        view[...] = view[...] + buf[...]

    def xy1(self):
        at = self.at
        for i, k in enumerate((at.kd, at.kx, at.ky, at.k)):
            self.d_copy(i).wait_recv()
            self.add(self.part(k, at.c), self.rd.at[i])
        for i in (ZERO, TWO, ONE, 3):
            self.xy1_copy(i).start()

    def xy2(self):
        at = self.at
        for i, (k, h) in ((ONE, (at.ky, ZERO)), (3, (at.kx, ONE)), (ZERO, (at.k, ZERO)), (TWO, (at.k, ONE))):
            self.xy1_copy(i).wait_recv()
            self.add(self.part(k, at.c, h), self.r1.at[i])
            if i == ONE:
                self.xy2_copy(ZERO).start()
            if i == 3:
                self.xy2_copy(ONE).start()

    def z1(self):
        at = self.at
        for i in range(TWO):
            self.xy2_copy(i).wait_recv()
            self.add(self.part(at.k, at.c, i), self.r2.at[i])
        for j in (ONE, ZERO, TWO):
            self.z1_copy(j).start()

    def z2(self):
        at = self.at
        rows, cols = self.quarter(at.z, pl.multiple_of(at.f * self.rows, 16))
        total = self.acc[rows, cols]
        for j in range(3):
            self.z1_copy(j).wait_recv()
            total = total + self.rz[j]
        rows, cols = self.quarter(at.z, ZERO)
        self.out[rows, cols] = total.astype(BF16)
        for j in (ONE, ZERO, TWO):
            self.z2_copy(j).start()

    def finish(self):
        for j in range(3):
            self.z2_copy(j).wait_recv()

    def drain(self):
        for i in range(4):
            self.d_copy(i).wait_send()
            self.xy1_copy(i).wait_send()
        for i in range(TWO):
            self.xy2_copy(i).wait_send()
        for i in range(3):
            self.z1_copy(i).wait_send()
            self.z2_copy(i).wait_send()

class Paired(Reduce):

    def piece(self, base, i, n):
        if self.rows == 48:
            return (pl.ds(pl.multiple_of(base, 16), self.rows), pl.ds(pl.multiple_of(i * 128, 128), n * 128))
        q = self.rows // 4
        return (pl.ds(pl.multiple_of(base + i * q, 16), n * q), slice(None))

    def y_copy(self):
        at = self.at
        rows, cols = self.piece(at.f * self.rows, TWO * (ONE - at.za), TWO)
        return self.copy(self.acc.at[rows, cols], self.rz[ZERO], 10, at.n1)

    def w_copy(self):
        at = self.at
        rows, cols = self.piece(at.f * self.rows, TWO * at.za + ONE - at.zb, ONE)
        return self.copy(self.acc.at[rows, cols], self.rz[ONE], 11, at.n2)

    def z_copy(self):
        at = self.at
        rows, cols = self.piece(ZERO, TWO * at.za + at.zb, ONE)
        v = self.out.at[rows, cols]
        return self.copy(v, v, 12, at.n2)

    def x_copy(self):
        at = self.at
        rows, cols = self.piece(ZERO, TWO * at.za, TWO)
        v = self.out.at[rows, cols]
        return self.copy(v, v, 13, at.n1)

    def z1(self):
        at = self.at
        for i in range(TWO):
            self.xy2_copy(i).wait_recv()
            self.add(self.part(at.k, at.c, i), self.r2.at[i])
        self.y_copy().start()

    def w1(self):
        at = self.at
        self.y_copy().wait_recv()
        rows, cols = self.piece(at.f * self.rows, TWO * at.za, TWO)
        self.add(self.acc.at[rows, cols], self.rz[ZERO])
        self.w_copy().start()

    def z2(self):
        at = self.at
        self.w_copy().wait_recv()
        rows, cols = self.piece(at.f * self.rows, TWO * at.za + at.zb, ONE)
        total = self.acc[rows, cols] + self.rz[ONE][...]
        rows, cols = self.piece(ZERO, TWO * at.za + at.zb, ONE)
        self.out[rows, cols] = total.astype(BF16)
        self.z_copy().start()

    def x2(self):
        self.z_copy().wait_recv()
        self.x_copy().start()

    def finish(self):
        self.x_copy().wait_recv()

    def drain_acc(self):
        for i in range(4):
            self.d_copy(i).wait_send()
            self.xy1_copy(i).wait_send()
        for i in range(TWO):
            self.xy2_copy(i).wait_send()
        self.y_copy().wait_send()
        self.w_copy().wait_send()

    def drain_out(self):
        self.z_copy().wait_send()
        self.x_copy().wait_send()

    def drain(self):
        self.drain_acc()
        self.drain_out()

class Small:

    def __init__(self, at, sm, smr, smk, smz, send, recv):
        self.at, self.sm, self.smr, self.smk, self.smz, self.send, self.recv = (at, sm, smr, smk, smz, send, recv)
        self.base = NG * NSEM

    def pair(self):
        return remote(self.sm, self.smr, self.send, self.recv, self.base, self.at.sib)

    def plane(self, j):
        v = self.smk.at[self.at.k]
        return remote(v, v, self.send, self.recv, self.base + ONE + j, (self.at.nd, self.at.nx, self.at.ny)[j])

    def stack(self, j):
        v = self.smz.at[self.at.z]
        return remote(v, v, self.send, self.recv, self.base + 4 + j, self.at.nz[j])

    def advance(self, i):
        if i == ZERO:
            self.pair().start()
        if i == ONE:
            self.pair().wait_recv()
            self.smk[self.at.k] = self.sm[...] + self.smr[...]
            for j in range(3):
                self.plane(j).start()
        if i == TWO:
            for j in range(3):
                self.plane(j).wait_recv()
            self.smz[self.at.z] = self.smk[ZERO] + self.smk[ONE] + (self.smk[TWO] + self.smk[3])
            for j in range(3):
                self.stack(j).start()

    def finish(self):
        for j in range(3):
            self.stack(j).wait_recv()
        return self.smz[ZERO] + self.smz[ONE] + (self.smz[TWO] + self.smz[3])

    def drain(self):
        self.pair().wait_send()
        for j in range(3):
            self.plane(j).wait_send()
            self.stack(j).wait_send()

def layer_kernel(x_hbm, pos_ref, seg_ref, relb_ref, ga_ref, gm_ref, wq_ref, wk_ref, wv_ref, wo_ref, wi0_ref, wi1_ref, wf_ref, go_hbm, y_hbm, small_ref, dq_ref, dk_ref, dv_ref, do_ref, di0_ref, di1_ref, df_ref, tab_s, pad_s, ga_s, gm_s, wqkv_s, wo_s, wi_s, wf_s, wqkvt_s, wot_s, wit_s, wft_s, xt_s, qkv_s, p_s, ctx_s, got_s, ut_s, zt_s, dgu_s, dh_s, dga_s, dgm_s, io_s, idx_s, *more):
    (acc, rd, r1, r2, rz, out, rq), more = ([more[i * NG:(i + ONE) * NG] for i in range(7)], more[7 * NG:])
    sm_s, smr_s, smk_s, smz_s, io_sem, out_sem, ag_own, ag_send, ag_recv, rs_send, rs_recv = more
    at = Place()
    barrier = pltpu.get_barrier_semaphore()
    peers = [at.sib, at.nx, at.ny, at.nd] + at.nz
    for dev in peers:
        pl.semaphore_signal(barrier, inc=ONE, device_id=dev, device_id_type=MESH)

    def rows_of(r):
        return pl.ds(pl.multiple_of(r * SEQ, SEQ), SEQ)

    def x_copy(r):
        return pltpu.make_async_copy(x_hbm.at[rows_of(r), :], io_s.at[rows_of(r), :], io_sem.at[ZERO, r])

    def go_copy(r):
        return pltpu.make_async_copy(go_hbm.at[rows_of(r), :], io_s.at[rows_of(r), :], io_sem.at[ONE, r])

    def y_copy(r):
        return pltpu.make_async_copy(io_s.at[rows_of(r), :], y_hbm.at[rows_of(r), :], io_sem.at[TWO, r])
    gather = Gather(at, (wq_ref, wk_ref, wv_ref, wo_ref, wi0_ref, wi1_ref, wf_ref), ((wqkv_s, ZERO), (wqkv_s, AW), (wqkv_s, TWO * AW), (wo_s, ZERO), (wi_s, ZERO), (wi_s, FF), (wf_s, ZERO)), ag_own, ag_send, ag_recv)
    for w in range(7):
        gather.load(w).start()
    for r in range(ROWS):
        x_copy(r).start()
    pl.semaphore_wait(barrier, len(peers))
    first, rest = ((ZERO, ONE, TWO), (3, 4, 5, 6))
    gather.begin(first, (TWO, ZERO, ONE, 3))
    gather.begin(rest, (ZERO, ONE, 3))
    setup_small(relb_ref, ga_ref, gm_ref, tab_s, pad_s, ga_s, gm_s)
    dgm_s[...] = jnp.zeros_like(dgm_s)
    dga_s[...] = jnp.zeros_like(dga_s)

    def prep(r):
        x_copy(r).wait()
        prep_row(r, io_s, ga_s, xt_s, ut_s)
        go_copy(r).start()
    loop(ROWS, prep)

    def prep_go(r):
        go_copy(r).wait()
        got_s[:, tok_slice(r)] = io_s[tok_slice(r), :].T
    loop(ROWS, prep_go)
    loop(ROWS, lambda r: table_row(r, pos_ref, seg_ref, tab_s, idx_s, p_s))
    gather.relay(first)
    gather.finish(first)
    wqkvt_s[...] = wqkv_s[...].T
    loop(TOK // 512, lambda r: qkv_block(r, wqkvt_s, ut_s, qkv_s))

    def fwd(r):
        attn_fwd_row(r, tab_s, idx_s, qkv_s, p_s, ctx_s)

        @pl.when(r == ZERO)
        def _():
            gather.relay1((3, 4))

        @pl.when(r == TWO)
        def _():
            gather.relay1((5,))

        @pl.when(r == 3)
        def _():
            gather.relay1((6,))
            gather.relay2((3, 4))
    loop(ROWS, fwd)
    gather.relay2((5, 6))
    gather.finish((3, 4))
    wot_s[...] = wo_s[...].T
    wit_s[ZERO:FF, :] = wi_s[:, ZERO:FF].T
    gather.finish((5, 6))
    wit_s[FF:TWO * FF, :] = wi_s[:, FF:TWO * FF].T
    wft_s[...] = wf_s[...].T
    mlp_in_row(ZERO, gm_s, wot_s, xt_s, ctx_s, ut_s, dh_s)

    def mlp_up(r):
        mlp_up_row(r, gm_s, wot_s, wit_s, wf_s, xt_s, ctx_s, got_s, ut_s, zt_s, dgu_s, dh_s)
    loop(ROWS, mlp_up)
    red = []
    for a in range(NG):
        if a in PAIRED:
            red.append(Paired(a, at, acc[a], rd[a], r1[a], r2[a], (rz[a], rq[a]), out[a], rs_send, rs_recv))
        else:
            red.append(Reduce(a, at, acc[a], rd[a], r1[a], r2[a], rz[a], out[a], rs_send, rs_recv))
    small = Small(at, sm_s, smr_s, smk_s, smz_s, rs_send, rs_recv)

    def cols(c, n=256):
        return pl.ds(pl.multiple_of(c * n, n), n)
    names = {'d': 'd_send', 'a': 'xy1', 'b': 'xy2', 'y': 'z1', 'w': 'w1', 'z': 'z2', 'x': 'x2'}

    def run_step(step, g):
        getattr(red[g], names[step])()

    def fire(name, i):
        steps = PLAN.get(f'{name}{i}', '')
        for step, g in zip(steps[::TWO], steps[ONE::TWO]):
            run_step(step, int(g))

    def fire_at(name, i, n, base=ZERO):
        for k in range(base, base + n):
            if f'{name}{k}' in PLAN:
                pl.when(i == k)(functools.partial(fire, name, k))
    for i in range(TWO):

        def dwf(c, i=i):
            part = pl.ds(pl.multiple_of(c * 512, 512), 512)
            acc[i][part, :] = mm_nt(zt_s[part, :], got_s[256 * i:256 * i + 256, :])
        loop(TWO, dwf)
        fire('wf', i)
    for g in range(4):

        def dwi(c, g=g):
            acc[TWO + g][:, cols(c)] = mm_nt(ut_s[...], dgu_s[cols(c + TWO * g), :])
            fire_at('wi', c + TWO * g, TWO, TWO * g)
        loop(TWO, dwi)

    def mlp_down(r):
        mlp_down_row(r, gm_s, wi_s, got_s, dgu_s, dh_s, dgm_s)
        fire_at('down', r, ROWS)
    loop(ROWS, mlp_down)

    def dwo(c):
        acc[6][:, cols(c)] = mm_nt(ctx_s[...], dh_s[cols(c), :])
    loop(TWO, dwo)
    fire('wo', ZERO)

    def bwd(r):
        attn_bwd_row(r, ga_s, wo_s, xt_s, ut_s, qkv_s, p_s, dh_s, dgu_s)
        fire_at('bwd', r, ROWS)
    loop(ROWS, bwd)
    for i in range(3):
        acc[7 + i][...] = mm_nt(ut_s[...], dgu_s[AW * i:AW * i + AW, :])
        fire('wqkv', i)
    for g in range(TWO):
        red[g].drain_acc()
        acc[g][...] = jnp.zeros_like(acc[g])

    def tail(r):
        bias_row(r, pos_ref, p_s, acc)
        fire_at('tail', r, ROWS)
        gain_row(r, wqkv_s, xt_s, dgu_s, dga_s)
        fire_at('gain', r, ROWS)
    loop(ROWS, tail)
    db_s = p_s.at[ZERO, ZERO]
    db_s[...] = jnp.zeros_like(db_s)
    bias_sums(acc, db_s)
    sm_s[ZERO:ONE, ZERO:256] = jnp.sum(p_s[ZERO, ZERO].T, axis=ZERO, keepdims=True)
    sm_s[ZERO:ONE, 256:512] = jnp.zeros((ONE, 256), F32)
    sm_s[ONE:TWO, :] = jnp.sum(dga_s[...].T, axis=ZERO, keepdims=True)
    sm_s[TWO:3, :] = jnp.sum(dgm_s[...].T, axis=ZERO, keepdims=True)
    sm_s[3:8, :] = jnp.zeros((5, 512), F32)
    small.advance(ZERO)
    fire('head', ZERO)

    def emit_out(r):
        out_row(r, io_s, wft_s, got_s, zt_s)
        y_copy(r).start()
        pl.when(r == ONE)(lambda: small.advance(ONE))
        fire_at('yrow', r, ROWS)
    loop(ROWS, emit_out)
    small.advance(TWO)
    finals = [(df_ref, ZERO, 256), (df_ref, 256, 256), (di0_ref, ZERO, 512), (di0_ref, 512, 512), (di1_ref, ZERO, 512), (di1_ref, 512, 512), (do_ref, ZERO, 512), (dq_ref, ZERO, AW), (dk_ref, ZERO, AW), (dv_ref, ZERO, AW)]
    finals = [pltpu.make_async_copy(out[g], dst.at[:, pl.ds(c, n)], out_sem.at[g]) for g, (dst, c, n) in enumerate(finals)]
    for g in range(NG):
        red[g].finish()
        finals[g].start()
    small_ref[...] = small.finish()
    for copy in finals:
        copy.wait()
    for r in range(ROWS):
        y_copy(r).wait()
    gather.drain(first, False)
    gather.drain(rest, True)
    for g in red[:TWO]:
        g.drain_out()
    for g in red[TWO:]:
        g.drain()
    small.drain()

def emit_kernel(y_in, small_ref, g0, g1, g2, g3, g4, g5, g6, y_out, db_ref, dga_ref, dgm_ref, o0, o1, o2, o3, o4, o5, o6, y_s, b0, b1, b2, b3, b4, b5, b6, in_sem, out_sem):
    pairs = [(y_in.at[pl.ds(r * SEQ, SEQ), :], y_s.at[pl.ds(r * SEQ, SEQ), :], y_out.at[pl.ds(r * SEQ, SEQ), :]) for r in range(ROWS)]
    pairs += list(zip((g0, g1, g2, g3, g4, g5, g6), (b0, b1, b2, b3, b4, b5, b6), (o0, o1, o2, o3, o4, o5, o6)))
    ins = [pltpu.make_async_copy(a, b, in_sem.at[i]) for i, (a, b, _) in enumerate(pairs)]
    outs = [pltpu.make_async_copy(b, c, out_sem.at[i]) for i, (_, b, c) in enumerate(pairs)]
    for copy in ins:
        copy.start()
    for h in range(HEADS):
        db_ref[h:h + ONE, :] = small_ref[ZERO:ONE, h * 32:(h + ONE) * 32]
    dga_ref[...] = small_ref[ONE:TWO, :]
    dgm_ref[...] = small_ref[TWO:3, :]
    for i in range(len(pairs)):
        ins[i].wait()
        outs[i].start()
    for copy in outs:
        copy.wait()

def local_layer(x_in, positions, segments, rel_bias, gain_attn, gain_mlp, wq, wk, wv, wo, wi0, wi1, wf, grad_out):
    vmem = pl.BlockSpec(memory_space=pltpu.VMEM)
    hbm = pl.BlockSpec(memory_space=pl.ANY)

    def bufs(shape_of, dtype):
        return [pltpu.VMEM(shape_of(r, c), dtype) for r, c in SHARD]

    def landing(a):
        r, c = SHARD[a]
        if a not in PAIRED:
            return ((3, r, 128) if r == 48 else (3, r // 4, c), (8, 128))
        return ((r, 256), (r, 128)) if r == 48 else ((r // TWO, c), (r // 4, c))
    outs = pl.pallas_call(layer_kernel, out_shape=[jax.ShapeDtypeStruct((TOK, DM), BF16), jax.ShapeDtypeStruct((8, 512), F32)] + [jax.ShapeDtypeStruct(w.shape, BF16) for w in (wq, wk, wv, wo, wi0, wi1, wf)], in_specs=[hbm] + [vmem] * 5 + [hbm] * 8, out_specs=[hbm, vmem] + [hbm] * 7, scratch_shapes=[pltpu.VMEM((8, 128), F32), pltpu.VMEM((128, 128), F32), pltpu.VMEM((DM, 128), F32), pltpu.VMEM((DM, 128), F32), pltpu.VMEM((DM, 3 * AW), BF16), pltpu.VMEM((AW, DM), BF16), pltpu.VMEM((DM, TWO * FF), BF16), pltpu.VMEM((FF, DM), BF16), pltpu.VMEM((3 * AW, DM), BF16), pltpu.VMEM((DM, AW), BF16), pltpu.VMEM((TWO * FF, DM), BF16), pltpu.VMEM((DM, FF), BF16), pltpu.VMEM((DM, TOK), BF16), pltpu.VMEM((3 * AW, TOK), BF16), pltpu.VMEM((HEADS, ROWS, SEQ, SEQ), F32), pltpu.VMEM((AW, TOK), BF16), pltpu.VMEM((DM, TOK), BF16), pltpu.VMEM((DM, TOK), BF16), pltpu.VMEM((FF, TOK), BF16), pltpu.VMEM((TWO * FF, TOK), BF16), pltpu.VMEM((DM, TOK), BF16), pltpu.VMEM((DM, 128), F32), pltpu.VMEM((DM, 128), F32), pltpu.VMEM((TOK, DM), BF16), pltpu.VMEM((ROWS, SEQ, SEQ), jnp.int32)] + bufs(lambda r, c: (8 * r, c), F32) + bufs(lambda r, c: (4, r, c), F32) + bufs(lambda r, c: (4, r // TWO, c), F32) + bufs(lambda r, c: (TWO, r // TWO, c), F32) + [pltpu.VMEM(landing(a)[ZERO], F32) for a in range(NG)] + bufs(lambda r, c: (r, c), BF16) + [pltpu.VMEM(landing(a)[ONE], F32) for a in range(NG)] + [pltpu.VMEM((8, 512), F32), pltpu.VMEM((8, 512), F32), pltpu.VMEM((4, 8, 512), F32), pltpu.VMEM((4, 8, 512), F32), pltpu.SemaphoreType.DMA((3, ROWS)), pltpu.SemaphoreType.DMA((NG,)), pltpu.SemaphoreType.DMA((7,)), pltpu.SemaphoreType.DMA((63,)), pltpu.SemaphoreType.DMA((63,)), pltpu.SemaphoreType.DMA((NG * NSEM + 7,)), pltpu.SemaphoreType.DMA((NG * NSEM + 7,))], compiler_params=pltpu.CompilerParams(vmem_limit_bytes=67043328, collective_id=ZERO, has_side_effects=True), name='layer')(x_in.reshape(TOK, DM), positions, segments, rel_bias.T, gain_attn.reshape(ONE, DM), gain_mlp.reshape(ONE, DM), wq, wk, wv, wo, wi0, wi1, wf, grad_out.reshape(TOK, DM))
    weights = (wq, wk, wv, wo, wi0, wi1, wf)
    outs = pl.pallas_call(emit_kernel, out_shape=[jax.ShapeDtypeStruct((TOK, DM), BF16), jax.ShapeDtypeStruct((HEADS, 32), F32), jax.ShapeDtypeStruct((ONE, DM), F32), jax.ShapeDtypeStruct((ONE, DM), F32)] + [jax.ShapeDtypeStruct(w.shape, BF16) for w in weights], in_specs=[hbm, vmem] + [hbm] * 7, out_specs=[hbm, vmem, vmem, vmem] + [hbm] * 7, scratch_shapes=[pltpu.VMEM((TOK, DM), BF16)] + [pltpu.VMEM(w.shape, BF16) for w in weights] + [pltpu.SemaphoreType.DMA((ROWS + 7,)), pltpu.SemaphoreType.DMA((ROWS + 7,))], name='emit')(*outs)
    y, db, dga, dgm = outs[:4]
    return (y.reshape(ROWS, SEQ, DM), db.T, dga.reshape(DM), dgm.reshape(DM)) + tuple(outs[4:])

def solution(mesh):
    row_spec = P(ROW_AXES)
    whole = P()
    part_spec = P('fsdp')
    in_specs = (row_spec, row_spec, row_spec, whole, whole, whole) + (part_spec,) * 7 + (row_spec,)
    out_specs = (row_spec, whole, whole, whole) + (part_spec,) * 7
    return jax.shard_map(local_layer, mesh=mesh, in_specs=in_specs, out_specs=out_specs, check_vma=False)
```

time: 109 us -> 107 us (0.982)
  Pallas kernels: 108 us -> 106 us
    pallas_call x1, Pallas kernels: 104 us -> 102 us  [local_layer(): pl.pallas_call(layer_kernel, out_shape=[jax.ShapeDtypeStruct((TOK, DM), B...]
where the time goes in v4:
time: 107 us
  Pallas kernels  106 us (99%)
    pallas_call x1, Pallas kernels, local_layer(): pl.pallas_call(layer_kernel, out_shape=[jax.ShapeDtypeStruct((TOK, DM), B...  102 us
    pallas_call x1, Pallas kernels, local_layer(): pl.pallas_call(emit_kernel, out_shape=[jax.ShapeDtypeStruct((TOK, DM), BF...  3.83 us

profile of v4, /device:TPU:0, one launch (start us, length us, event | category | flops | bytes accessed | tf_op | source)
XLA Modules:
  0.0 107.0 jit_solution(5997383677275822496)
XLA Ops:
  0.6 102.4 %layer.1 = (bf16[1536,512]{1,0:T(8,128)(2,1)}, f32[8,512]{1,0:T(8,128)}, bf16[64,384]{1,0:T(8,128)(2,1)}, bf16[64,384]{1,0:T(8,128)(2,1)}, bf16[64,384]{1,0:T(8,...) custom-call(bf16[1536,512]{1,0:T(8,128)(2,1)} %bitcast.9, ...), custom_call_target="tpu_custom_call" | custom-call | tf_op jit(solution)/shard_map/layer/pallas_call | solution.py:780
  103.0 3.8 %emit.1 = (bf16[1536,512]{1,0:T(8,128)(2,1)}, f32[6,32]{1,0:T(8,128)}, f32[1,512]{1,0:T(1,128)}, f32[1,512]{1,0:T(1,128)}, bf16[64,384]{1,0:T(8,128)(2,1)}, /*in...) custom-call(bf16[1536,512]{1,0:T(8,128)(2,1)} %get-tuple-element.31., ...), custom_call_target="tpu_custom_call" | custom-call | tf_op jit(solution)/shard_map/emit/pallas_call | solution.py:782
